TPU v7x, 256 devices: a 2x2x32 block of a 4x8x32 slice. The times are simulated.
256 devices in a mesh: grp: 4 (over x, y), ep: 64 (over z, core).
Axes of the slice: x: 2, y: 2, z: 32, core: 2. Of those that a mesh axis runs over, the one named last changes fastest.
The devices are a block of a 4x8x32 slice.
Arguments:
- expert_ids: int32 [16384, 8], P(('grp', 'ep')), parts along dimension 0, may hold values from 0 to 63, all different within a row; in each aligned block of 64 rows (0 to 63, 64 to 127, ...) at most 16 rows name the same one
- route_gates: float32 [16384, 8], P(('grp', 'ep')), parts along dimension 0, may hold values from 0.1 to 0.5
- routed_in: bfloat16 [16384, 8, 2048], P(('grp', 'ep')), parts along dimension 0, may hold values from -6 to 6
- down_weight: bfloat16 [64, 1024, 3584], P('ep'), may hold values from -0.1875 to 0.1875
- slot_offset: int32 [1], replicated, may hold values from 0 to 63
Outputs:
- combined: bfloat16 [16384, 3584], P(('grp', 'ep')), parts along dimension 0
There are 4 independent parts, one for each index of `grp`. A program takes and returns all parts, laid end to end along the dimension named above; an argument that names none is the same for every part. Nothing has to cross between parts.
Inputs may be any that keep to these rules, and one draw needn't show every extreme that they name: `expert_ids`: each row names 8 different experts. Among the tokens of one ep device, no expert is named by more than 16 tokens, a bound that some block reaches in some devices.
All inputs are finite; a program needn't handle non-finite values.
Results may differ from a plain program's by a relative error of at most 0.0057.
Values may be sent and summed in bfloat16 or wider, within the bound.
No kernel may reach another device: no remote copies, remote signals or barrier semaphores. Data moves between devices by JAX's collectives and lax.ppermute only.
A program may use at most 128 MiB of HBM per device.

v0:
```python
import jax
import jax.numpy as jnp
from jax import lax
from jax.sharding import PartitionSpec as P


def swiglu(packed):
    half = packed.shape[-1] // 2
    gate = packed[..., :half].astype(jnp.float32)
    upper = packed[..., half:].astype(jnp.float32)
    return (jax.nn.silu(gate) * upper).astype(jnp.bfloat16)


def on_device(expert_ids, route_gates, routed_in, down_weight, slot_offset):
    experts = lax.axis_size("ep")
    tokens_here, chosen = expert_ids.shape
    pair_count = tokens_here * chosen
    capacity = 2 * pair_count // experts
    matrix = down_weight[0]
    offset = slot_offset[0]
    target = jnp.mod(expert_ids.reshape(pair_count) - offset, experts)
    onehot = (target[:, None] == jnp.arange(experts, dtype=jnp.int32)[None, :]).astype(jnp.int32)
    earlier = jnp.cumsum(onehot, axis=0) - onehot
    rank = jnp.sum(earlier * onehot, axis=1)
    row_index = target * capacity + rank
    source = (
        jnp.full((experts * capacity,), pair_count, jnp.int32)
        .at[row_index]
        .set(jnp.arange(pair_count, dtype=jnp.int32))
    )
    payload = routed_in.reshape(pair_count, routed_in.shape[2])
    payload = swiglu(payload)
    padded = jnp.concatenate([payload, jnp.zeros((1, payload.shape[1]), jnp.bfloat16)], axis=0)
    outgoing = jnp.take(padded, source, axis=0).reshape(experts, capacity, payload.shape[1])
    results = jnp.einsum(
        "nkf,fd->nkd",
        lax.all_to_all(outgoing, "ep", split_axis=0, concat_axis=0, tiled=True),
        matrix,
        preferred_element_type=jnp.float32,
    ).astype(jnp.bfloat16)
    returned = lax.all_to_all(results, "ep", split_axis=0, concat_axis=0, tiled=True)
    width = returned.shape[2]
    picked = jnp.take(returned.reshape(experts * capacity, width), row_index, axis=0).reshape(
        tokens_here, chosen, width
    )
    total = jnp.zeros((tokens_here, width), jnp.float32)
    for choice_index in range(chosen):
        total = total + route_gates[:, choice_index, None] * picked[:, choice_index].astype(
            jnp.float32
        )
    return total.astype(jnp.bfloat16)


def solution(mesh):
    placed = (
        P(("grp", "ep"), None),
        P(("grp", "ep"), None),
        P(("grp", "ep"), None, None),
        P("ep", None, None),
        P(),
    )
    return jax.shard_map(
        on_device, mesh=mesh, in_specs=placed, out_specs=P(("grp", "ep"), None), check_vma=False
    )
```

profile of v0, /device:TPU:37, one launch (start us, length us, event | category | flops | bytes accessed | tf_op | source)
XLA Modules:
  0.0 920.6 jit_solution(13544566188059349619)
XLA Ops:
  0.7 0.7 broadcast_subtract_fusion
  1.3 0.1 copy.11
  1.4 0.1 sub.35
  1.5 0.1 sub.34
  1.6 0.1 sub.37
  1.7 1.2 reduce-window.6
  2.9 0.2 slice_reduce_fusion
  3.2 0.1 fusion.16
  3.4 2.4 scatter_custom_fusion
  5.9 2.2 fusion.5
  8.1 0.1 broadcast_in_dim.33
  8.2 0.1 concatenate.3
  8.3 4.1 gather_fusion
  12.3 0.3 broadcast_select_fusion
  12.6 231.5 %all_to_all.10 = bf16[64,16,1024]{2,1,0:T(8,128)(2,1)S(1)} all-to-all(bf16[64,16,1024]{2,1,0:T(8,128)(2,1)S(1)} %broadcast_select_fusion), channel_id=1, replica_groups=mesh['grp'=4,'ep'=64] {'ep'}, dimensions={0} | all-to-all | bytes 4194304 | tf_op jit(solution)/shard_map/all_to_all | solution.py:37
  244.1 13.0 %convolution_convert_fusion = bf16[64,16,3584]{2,1,0:T(8,128)(2,1)} fusion(bf16[64,16,1024]{2,1,0:T(8,128)(2,1)S(1)} %all_to_all.10, bf16[1,1024,3584]{2,1,0:T(8,128)(2,1)} %param.8), kind=kOutput, calls=%fused_computation.3 | convolution fusion | flops 7519862784 | bytes 16777216 | tf_op jit(solution)/shard_map/nkf,fd->nkd/dot_general | solution.py:35
  257.1 0.0 copy-start.1
  257.1 0.0 copy-start
  257.1 8.9 all-to-all-start.1
  265.9 0.1 reduce_sum.14
  266.0 0.1 copy.14
  266.1 0.0 copy-done.1
  266.1 0.0 copy-done
  266.2 636.4 %all-to-all-done.1 = bf16[64,16,3584]{2,1,0:T(8,128)(2,1)} async-done(((bf16[64,16,3584]{2,1,0:T(8,128)(2,1)}), bf16[64,16,3584]{2,1,0:T(8,128)(2,1)}, u32[]{:S(2)}, u32[]{:S(2)}) %all-to-all-start.1) | async-done | bytes 7340064 | tf_op jit(solution)/shard_map/all_to_all | solution.py:41
  902.6 11.9 %gather_fusion.1 = bf16[512,3584]{1,0:T(8,128)(2,1)} fusion(bf16[1024,3584]{1,0:T(8,128)(2,1)} %bitcast.9, s32[1024]{0:T(1024)S(1)} %pad_clamp_fusion), kind=kCustom, calls=%fused_computation.1 | custom fusion | bytes 7342080 | tf_op jit(solution)/shard_map/jit(_take)/gather | solution.py:43
  914.5 4.4 copy_select_fusion
  918.9 1.7 fusion.7
  (12 shorter events, 0.1 us)
Async XLA Ops:
  257.1 9.0 copy-start.1
  257.1 9.1 copy-start
  257.1 645.5 %all-to-all-start.1 = ((bf16[64,16,3584]{2,1,0:T(8,128)(2,1)}), bf16[64,16,3584]{2,1,0:T(8,128)(2,1)}, u32[]{:S(2)}, u32[]{:S(2)}) async-start(bf16[64,16,3584]{2,1,0:T(8,128)(2,1)} %convolution_convert_fusion), calls=%async_computation.1 | async-start | bytes 14680064 | tf_op jit(solution)/shard_map/all_to_all | solution.py:41
where the time goes:
time: 933 us; the launch traced here: 921 us
  waiting for transfers between devices  636 us (68%)
  blocking collectives  232 us (25%)
  local copies, waits for them, and re-layouts  19.4 us (2%)
  matrix products  13 us (1%)
  other arithmetic  10.7 us (1%)
    all_to_all x1, waiting for transfers between devices, on_device(): lax.all_to_all(results, 'ep', split_axis=0, concat_axis=0, tiled=True)  636 us
    all_to_all x1, blocking collectives, on_device(): lax.all_to_all(outgoing, 'ep', split_axis=0, concat_axis=0, tiled=True)  232 us
  transfers between devices with their start and end apart: 1, of which 1 were waited for; matrix products, arithmetic and copies ran while one was open for 0% of the time, Pallas kernels for 0%

commit v1 on v0

v1 whole, which is shorter than its diff:
```python
import jax
import jax.numpy as jnp
from jax import lax
from jax.experimental import pallas as pl
from jax.experimental.pallas import tpu as pltpu
from jax.sharding import PartitionSpec as P

CHAINS = 2
NO_TOKEN = 1024.0
INTERPRET = False


def exact_parts(value):
    high = value.astype(jnp.bfloat16).astype(jnp.float32)
    rest = value - high
    middle = rest.astype(jnp.bfloat16).astype(jnp.float32)
    return high, middle, rest - middle


def pack_kernel(target_ref, gate_ref, routed_ref, rows_ref, meta_ref, *, experts, capacity, chosen):
    pairs, width = routed_ref.shape
    half = width // 2
    target = target_ref[...]
    expert = lax.broadcasted_iota(jnp.int32, (experts, pairs), 0)
    before = lax.broadcasted_iota(jnp.int32, (pairs, pairs), 0) < lax.broadcasted_iota(
        jnp.int32, (pairs, pairs), 1
    )
    named = expert == target
    earlier = jnp.dot(
        named.astype(jnp.bfloat16), before.astype(jnp.bfloat16), preferred_element_type=jnp.float32
    )
    rank = jnp.sum(jnp.where(named, earlier, 0.0), axis=0, keepdims=True).astype(jnp.int32)
    slot = target * capacity + rank
    at_rank = (lax.broadcasted_iota(jnp.int32, (capacity, pairs), 0) == rank).astype(jnp.bfloat16)
    token = (lax.broadcasted_iota(jnp.int32, (1, pairs), 1) // chosen + 1).astype(jnp.float32)
    values = (token,) + exact_parts(gate_ref[...])
    partner = (expert ^ 1) == target
    for place, value in enumerate(values):
        for side, mask in enumerate((named, partner)):
            found = lax.dot_general(
                jnp.where(mask, value, 0.0).astype(jnp.bfloat16),
                at_rank,
                (((1,), (1,)), ((), ())),
                preferred_element_type=jnp.float32,
            )
            if place == 0:
                found = jnp.where(found > 0.0, found - 1.0, NO_TOKEN)
            start = (2 * place + side) * capacity
            meta_ref[:, start : start + capacity] = found
    gate = routed_ref[:, :half].astype(jnp.float32)
    upper = routed_ref[:, half:].astype(jnp.float32)
    hidden = (gate / (1.0 + jnp.exp(-gate)) * upper).astype(jnp.bfloat16)
    pick = (
        lax.broadcasted_iota(jnp.int32, (experts * capacity, pairs), 0) == slot
    ).astype(jnp.bfloat16)
    rows_ref[...] = jnp.dot(pick, hidden, preferred_element_type=jnp.float32).astype(jnp.bfloat16)


def expert_kernel(place_ref, *refs, homes, chips, tokens):
    count = len(homes)
    own_rows, other_rows = refs[:count], refs[count : 2 * count]
    own_weight, other_weight, token_ref, gate_ref, out_ref = refs[2 * count :]
    capacity, width = own_rows[0].shape[1:]

    def project(blocks, weight):
        rows = jnp.concatenate([b[...].reshape(2 * capacity, width) for b in blocks], axis=0)
        return jnp.dot(rows, weight[...], preferred_element_type=jnp.float32).astype(jnp.bfloat16)

    own = project(own_rows, own_weight)
    other = project(other_rows, other_weight)
    lanes = token_ref.shape[2]
    wanted = lax.broadcasted_iota(jnp.int32, (2 * tokens, lanes), 0).astype(jnp.float32)
    for place, home in enumerate(homes):
        chip = lax.rem(place_ref[0] + (home + chips), chips)
        base = place * 2 * capacity
        rows = []
        for side in range(2):
            lo = base + side * capacity
            rows.append(own[lo : lo + capacity])
            rows.append(other[lo : lo + capacity])
        stacked = jnp.concatenate(rows * 3, axis=0)
        scale = jnp.where(token_ref[chip] == wanted, gate_ref[chip], 0.0).astype(jnp.bfloat16)
        out_ref[0, place] = jnp.dot(scale, stacked, preferred_element_type=jnp.float32).astype(
            jnp.bfloat16
        )


def expert_call(place, own, other, own_weight, other_weight, token, gate, homes, chips, tokens):
    experts, capacity, width = own.shape
    columns = own_weight.shape[1] // 2
    piece = columns // CHAINS
    count = len(homes)

    def row_spec(home):
        return pl.BlockSpec(
            (2, capacity, width), lambda j, s, home=home: (lax.rem(s[0] + (home + chips), chips), 0, 0)
        )

    weight_spec = pl.BlockSpec((width, piece), lambda j, s: (0, s[1] * CHAINS + j))
    table_spec = pl.BlockSpec(token.shape, lambda j, s: (0, 0, 0))
    grid_spec = pltpu.PrefetchScalarGridSpec(
        num_scalar_prefetch=1,
        grid=(CHAINS,),
        in_specs=[row_spec(h) for h in homes] * 2 + [weight_spec] * 2 + [table_spec] * 2,
        out_specs=pl.BlockSpec((1, count, 2 * tokens, piece), lambda j, s: (j, 0, 0, 0)),
    )
    return pl.pallas_call(
        lambda *refs: expert_kernel(*refs, homes=homes, chips=chips, tokens=tokens),
        grid_spec=grid_spec,
        out_shape=jax.ShapeDtypeStruct((CHAINS, count, 2 * tokens, piece), jnp.bfloat16),
        compiler_params=pltpu.CompilerParams(
            dimension_semantics=("arbitrary",), vmem_limit_bytes=32 * 1024 * 1024
        ),
        interpret=INTERPRET,
    )(place, *([own] * count), *([other] * count), own_weight, other_weight, token, gate)


def add_kernel(left_ref, right_ref, out_ref):
    def some(i, carry):
        at = pl.ds(pl.multiple_of(i * 16, 16), 16)
        total = left_ref[at].astype(jnp.float32) + right_ref[0, 0, at].astype(jnp.float32)
        out_ref[at] = total.astype(jnp.bfloat16)
        return carry

    lax.fori_loop(0, out_ref.shape[0] // 16, some, 0)


def add_own(arrived, batch, chain, place):
    return pl.pallas_call(
        add_kernel,
        grid=(1,),
        in_specs=[
            pl.BlockSpec(arrived.shape, lambda i: (0, 0)),
            pl.BlockSpec((1, 1) + arrived.shape, lambda i: (chain, place, 0, 0)),
        ],
        out_specs=pl.BlockSpec(arrived.shape, lambda i: (0, 0)),
        out_shape=jax.ShapeDtypeStruct(arrived.shape, jnp.bfloat16),
        compiler_params=pltpu.CompilerParams(vmem_limit_bytes=4 * 1024 * 1024),
        interpret=INTERPRET,
    )(arrived, batch)


def on_device(expert_ids, route_gates, routed_in, down_weight, slot_offset):
    experts = lax.axis_size("ep")
    chips = experts // 2
    tokens, chosen = expert_ids.shape
    pairs = tokens * chosen
    capacity = 2 * pairs // experts
    hidden_width = routed_in.shape[2] // 2
    weight = down_weight[0]
    width = weight.shape[1]
    index = lax.axis_index("ep")
    core = lax.rem(index, 2)
    place = jnp.stack([index // 2, core]).astype(jnp.int32)
    swap = [(i, i ^ 1) for i in range(experts)]
    onward = [(i, (i + 2) % experts) for i in range(experts)]
    backward = [(i, (i - 2) % experts) for i in range(experts)]

    partner_weight = lax.ppermute(weight, "ep", swap)
    target = jnp.mod(expert_ids - slot_offset[0], experts).reshape(1, pairs)
    rows, meta = pl.pallas_call(
        lambda *refs: pack_kernel(*refs, experts=experts, capacity=capacity, chosen=chosen),
        out_shape=(
            jax.ShapeDtypeStruct((experts * capacity, hidden_width), jnp.bfloat16),
            jax.ShapeDtypeStruct((experts, 8 * capacity), jnp.float32),
        ),
        compiler_params=pltpu.CompilerParams(vmem_limit_bytes=32 * 1024 * 1024),
        interpret=INTERPRET,
    )(target, route_gates.reshape(1, pairs), routed_in.reshape(pairs, 2 * hidden_width))
    meta = lax.all_to_all(meta, "ep", split_axis=0, concat_axis=0, tiled=True)
    own_rows = lax.all_to_all(
        rows.reshape(experts, capacity, hidden_width), "ep", split_axis=0, concat_axis=0, tiled=True
    )
    other_rows = lax.ppermute(own_rows, "ep", swap)

    meta = meta.reshape(chips, 2, 4, 2 * capacity).transpose(0, 2, 1, 3)
    token = meta[:, 0] + (tokens * jnp.arange(2, dtype=jnp.float32))[None, :, None]
    token = jnp.tile(token.reshape(chips, 1, 4 * capacity), (1, 1, 3))
    gate = meta[:, 1:].reshape(chips, 1, 12 * capacity)

    half = chips // 2
    batch = 4
    sums = {}
    for first in range(0, half, batch):
        homes = [half - s for s in range(first, first + batch)]
        homes += [s + 1 - half for s in range(first, first + batch)]
        out = expert_call(
            place, own_rows, other_rows, weight, partner_weight, token, gate, homes, chips, tokens
        )
        for i, home in enumerate(homes):
            sums[home] = (out, i)

    def own_sum(home, c):
        batch, i = sums[home]
        return batch[c, i]

    def with_own(arrived, home, c):
        batch, i = sums[home]
        return add_own(arrived, batch, c, i)

    ahead = [own_sum(half, c) for c in range(CHAINS)]
    behind = [own_sum(1 - half, c) for c in range(CHAINS)]
    for step in range(half):
        for c in range(CHAINS):
            ahead[c] = lax.ppermute(ahead[c], "ep", onward)
            if step < half - 1:
                behind[c] = lax.ppermute(behind[c], "ep", backward)
                ahead[c] = with_own(ahead[c], half - 1 - step, c)
            if step < half - 2:
                behind[c] = with_own(behind[c], step + 2 - half, c)

    done = jnp.concatenate(
        [
            (
                ahead[c].astype(jnp.float32)
                + behind[c].astype(jnp.float32)
                + own_sum(0, c).astype(jnp.float32)
            ).astype(jnp.bfloat16)
            for c in range(CHAINS)
        ],
        axis=1,
    ).reshape(2, tokens, width // 2)
    kept = lax.dynamic_index_in_dim(done, core, 0, keepdims=False)
    given = lax.dynamic_index_in_dim(done, 1 - core, 0, keepdims=False)
    taken = lax.ppermute(given, "ep", swap)
    low = jnp.where(core == 0, kept, taken)
    high = jnp.where(core == 0, taken, kept)
    return jnp.concatenate([low, high], axis=1)


def solution(mesh):
    placed = (
        P(("grp", "ep"), None),
        P(("grp", "ep"), None),
        P(("grp", "ep"), None, None),
        P("ep", None, None),
        P(),
    )
    return jax.shard_map(
        on_device, mesh=mesh, in_specs=placed, out_specs=P(("grp", "ep"), None), check_vma=False
    )
```

time: 933 us -> 473 us (0.51)
  waiting for transfers between devices: 636 us -> 278 us
  blocking collectives: 232 us -> 0 us
  starting transfers between devices: 8.86 us -> 139 us
  Pallas kernels: 0 us -> 31.9 us
  matrix products: 13 us -> 0 us
  local copies, waits for them, and re-layouts: 19.4 us -> 8.41 us
    all_to_all x1 -> x2, waiting for transfers between devices: 636 us -> 218 us  [the longest x1 196 us: on_device(): lax.all_to_all(rows.reshape(experts, capacity, hidden_width), 'ep', split...]
    all_to_all x1 -> x0, blocking collectives: 232 us -> none  [on_device(): lax.all_to_all(outgoing, 'ep', split_axis=0, concat_axis=0, tiled=True)]
    ppermute x0 -> x65, starting transfers between devices: none -> 99.8 us  [the longest x30 72.8 us: on_device(): behind[c] = lax.ppermute(behind[c], 'ep', backward)]
    ppermute x0 -> x65, waiting for transfers between devices: none -> 60.3 us  [the longest x32 40 us: on_device(): ahead[c] = lax.ppermute(ahead[c], 'ep', onward)]
    pallas_call x0 -> x63, Pallas kernels: none -> 31.9 us  [the longest x4 24.8 us: expert_call(): pl.pallas_call(lambda *refs: expert_kernel(*refs, homes=homes, chips=chip...]
    all_to_all x1 -> x2, starting transfers between devices: 8.86 us -> 39.6 us  [the longest x1 34.3 us: on_device(): lax.all_to_all(rows.reshape(experts, capacity, hidden_width), 'ep', split...]
    gather x2 -> x0, local copies, waits for them, and re-layouts: 16 us -> none  [the longest x1 11.9 us: on_device(): jnp.take(returned.reshape(experts * capacity, width), row_index, axis=0)]
    dot_general x1 -> x0, matrix products: 13 us -> none  [on_device(): jnp.einsum('nkf,fd->nkd', lax.all_to_all(outgoing, 'ep', split_axis=0, co...]
  transfers between devices with their start and end apart: 1 -> 67, of which waited for: 1 -> 32; matrix products, arithmetic and copies ran while one was open for 0% -> 0% of each run, Pallas kernels for 0% -> 5%
where the time goes in v1:
time: 473 us; the launch traced here: 464 us
  waiting for transfers between devices  278 us (59%)
  starting transfers between devices  139 us (29%)
  Pallas kernels  31.9 us (7%)
  local copies, waits for them, and re-layouts  8.41 us (2%)
    all_to_all x1, waiting for transfers between devices, on_device(): lax.all_to_all(rows.reshape(experts, capacity, hidden_width), 'ep', split...  196 us
    ppermute x30, starting transfers between devices, on_device(): behind[c] = lax.ppermute(behind[c], 'ep', backward)  72.8 us
    ppermute x32, waiting for transfers between devices, on_device(): ahead[c] = lax.ppermute(ahead[c], 'ep', onward)  40 us
    all_to_all x1, starting transfers between devices, on_device(): lax.all_to_all(rows.reshape(experts, capacity, hidden_width), 'ep', split...  34.3 us
    pallas_call x4, Pallas kernels, expert_call(): pl.pallas_call(lambda *refs: expert_kernel(*refs, homes=homes, chips=chip...  24.8 us
    all_to_all x1, waiting for transfers between devices, on_device(): meta = lax.all_to_all(meta, 'ep', split_axis=0, concat_axis=0, tiled=True)  22.1 us
    ppermute x30, waiting for transfers between devices, on_device(): behind[c] = lax.ppermute(behind[c], 'ep', backward)  19.2 us
    ppermute x1, starting transfers between devices, on_device(): taken = lax.ppermute(given, 'ep', swap)  13.5 us
  transfers between devices with their start and end apart: 67, of which 32 were waited for; matrix products, arithmetic and copies ran while one was open for 0% of the time, Pallas kernels for 5%

profile of v1, /device:TPU:37, one launch (start us, length us, event | category | flops | bytes accessed | tf_op | source)
XLA Modules:
  0.0 463.7 jit_solution(13254409391534065864)
XLA Ops:
  7.1 34.3 %all-to-all-start = ((bf16[64,16,1024]{2,1,0:T(8,128)(2,1)}), bf16[64,16,1024]{2,1,0:T(8,128)(2,1)S(1)}, u32[]{:S(2)}, u32[]{:S(2)}) async-start(bf16[64,16,1024]{2,1,0:T(8,128)(2,1)} %bitcast.45), calls=%async_computation | async-start | bytes 4194304 | tf_op jit(solution)/shard_map/all_to_all | solution.py:171
  42.9 195.9 %all-to-all-done.refs_1_.refs_2_.refs_3_.refs_4_.refs_5_.refs_6_.refs_7_.refs_8_ = bf16[64,16,1024]{2,1,0:T(8,128)(2,1)S(1)} async-done(((bf16[64,16,1024]{2,1,0:T(8,128)(2,1)}), bf16[64,16,1024]{2,1,0:T(8,128)(2,1)S(1)}, u32[]{:S(2)}, u32[]{:S(2)}) %all-to-all-start) | async-done | bytes 2097184 | tf_op jit(solution)/shard_map/all_to_all | solution.py:171
  238.8 3.0 collective-permute-start
  241.8 5.2 %all-to-all-start.1 = ((f32[64,1,128]{2,1,0:T(1,128)}), f32[64,1,128]{2,1,0:T(1,128)S(1)}, u32[]{:S(2)}, u32[]{:S(2)}) async-start(f32[64,1,128]{2,1,0:T(1,128)} %bitcast.7), calls=%async_computation.1 | async-start | bytes 65536 | tf_op jit(solution)/shard_map/all_to_all | solution.py:170
  247.3 22.1 %all-to-all-done.1 = f32[64,1,128]{2,1,0:T(1,128)S(1)} async-done(((f32[64,1,128]{2,1,0:T(1,128)}), f32[64,1,128]{2,1,0:T(1,128)S(1)}, u32[]{:S(2)}, u32[]{:S(2)}) %all-to-all-start.1) | async-done | bytes 32800 | tf_op jit(solution)/shard_map/all_to_all | solution.py:170
  271.3 3.1 copy-done.1
  274.3 6.2 %shard_map.56.right_ref = bf16[2,8,128,896]{3,2,1,0:T(8,128)(2,1)S(1)} custom-call(s32[2]{0:T(128)S(1)} %pad_add_fusion.refs_0_, bf16[64,16,1024]{2,1,0:T(8,128)(2,1)S(1)} %all-to-all-done.refs_1_.refs_2_.refs_3_.refs_4_.refs_5_.refs_6_.refs_7_.refs_8_, bf16[64,16,1024]{2,1,0:T(8,128)(2,1)S(1)} %all-to-all-done.refs_1_.refs_2_.refs_3_.refs_4_.refs_5_.refs_6_.refs_7_.refs_8_, ...), custom_call_target="tpu_custom_call" | custom-call | tf_op jit(solution)/shard_map/pallas_call | solution.py:107
  280.9 2.6 collective-permute-start.49
  285.1 3.2 collective-permute-done.2.left_ref
  288.5 4.7 %collective-permute-done.33.left_ref = bf16[128,896]{1,0:T(8,128)(2,1)S(1)} collective-permute-done((bf16[128,896]{1,0:T(8,128)(2,1)S(1)}, bf16[128,896]{1,0:T(8,128)(2,1)S(1)}, u32[]{:S(2)}, u32[]{:S(2)}) %collective-permute-start.33) | collective-permute-done | bytes 229408 | tf_op jit(solution)/shard_map/ppermute | solution.py:205
  293.5 2.7 collective-permute-start.50
  298.2 4.7 %collective-permute-done.34.left_ref = bf16[128,896]{1,0:T(8,128)(2,1)S(1)} collective-permute-done((bf16[128,896]{1,0:T(8,128)(2,1)S(1)}, bf16[128,896]{1,0:T(8,128)(2,1)S(1)}, u32[]{:S(2)}, u32[]{:S(2)}) %collective-permute-start.34) | collective-permute-done | bytes 229408 | tf_op jit(solution)/shard_map/ppermute | solution.py:205
  303.3 2.7 collective-permute-start.51
  308.0 4.7 %collective-permute-done.35.left_ref = bf16[128,896]{1,0:T(8,128)(2,1)S(1)} collective-permute-done((bf16[128,896]{1,0:T(8,128)(2,1)S(1)}, bf16[128,896]{1,0:T(8,128)(2,1)S(1)}, u32[]{:S(2)}, u32[]{:S(2)}) %collective-permute-start.35) | collective-permute-done | bytes 229408 | tf_op jit(solution)/shard_map/ppermute | solution.py:205
  312.9 6.2 %shard_map.60.right_ref = bf16[2,8,128,896]{3,2,1,0:T(8,128)(2,1)S(1)} custom-call(s32[2]{0:T(128)S(1)} %pad_add_fusion.refs_0_, bf16[64,16,1024]{2,1,0:T(8,128)(2,1)S(1)} %all-to-all-done.refs_1_.refs_2_.refs_3_.refs_4_.refs_5_.refs_6_.refs_7_.refs_8_, bf16[64,16,1024]{2,1,0:T(8,128)(2,1)S(1)} %all-to-all-done.refs_1_.refs_2_.refs_3_.refs_4_.refs_5_.refs_6_.refs_7_.refs_8_, ...), custom_call_target="tpu_custom_call" | custom-call | tf_op jit(solution)/shard_map/pallas_call | solution.py:107
  319.3 2.7 collective-permute-start.52
  322.4 1.9 collective-permute-start.6
  325.1 3.2 collective-permute-start.53
  329.0 2.9 collective-permute-start.22
  334.0 3.4 collective-permute-start.54
  338.9 3.3 collective-permute-start.23
  343.8 3.3 collective-permute-start.55
  348.7 3.3 collective-permute-start.24
  352.2 2.1 collective-permute-done.39.left_ref
  354.7 6.2 %shard_map.65.right_ref = bf16[2,8,128,896]{3,2,1,0:T(8,128)(2,1)S(1)} custom-call(s32[2]{0:T(128)S(1)} %pad_add_fusion.refs_0_, bf16[64,16,1024]{2,1,0:T(8,128)(2,1)S(1)} %all-to-all-done.refs_1_.refs_2_.refs_3_.refs_4_.refs_5_.refs_6_.refs_7_.refs_8_, bf16[64,16,1024]{2,1,0:T(8,128)(2,1)S(1)} %all-to-all-done.refs_1_.refs_2_.refs_3_.refs_4_.refs_5_.refs_6_.refs_7_.refs_8_, ...), custom_call_target="tpu_custom_call" | custom-call | tf_op jit(solution)/shard_map/pallas_call | solution.py:107
  361.1 2.8 collective-permute-start.56
  366.9 3.2 collective-permute-start.57
  370.2 2.4 collective-permute-start.26
  373.4 1.9 collective-permute-done.41.left_ref
  375.7 2.7 collective-permute-start.58
  378.5 2.0 collective-permute-start.27
  381.3 4.7 %collective-permute-done.42.left_ref = bf16[128,896]{1,0:T(8,128)(2,1)S(1)} collective-permute-done((bf16[128,896]{1,0:T(8,128)(2,1)S(1)}, bf16[128,896]{1,0:T(8,128)(2,1)S(1)}, u32[]{:S(2)}, u32[]{:S(2)}) %collective-permute-start.42) | collective-permute-done | bytes 229408 | tf_op jit(solution)/shard_map/ppermute | solution.py:205
  386.3 3.0 collective-permute-start.59
  389.4 2.0 collective-permute-start.28
  391.6 2.6 collective-permute-done.43.left_ref
  394.5 6.2 %shard_map.70.right_ref = bf16[2,8,128,896]{3,2,1,0:T(8,128)(2,1)S(1)} custom-call(s32[2]{0:T(128)S(1)} %pad_add_fusion.refs_0_, bf16[64,16,1024]{2,1,0:T(8,128)(2,1)S(1)} %all-to-all-done.refs_1_.refs_2_.refs_3_.refs_4_.refs_5_.refs_6_.refs_7_.refs_8_, bf16[64,16,1024]{2,1,0:T(8,128)(2,1)S(1)} %all-to-all-done.refs_1_.refs_2_.refs_3_.refs_4_.refs_5_.refs_6_.refs_7_.refs_8_, ...), custom_call_target="tpu_custom_call" | custom-call | tf_op jit(solution)/shard_map/pallas_call | solution.py:107
  400.8 2.7 collective-permute-start.60
  405.7 2.9 collective-permute-done.60.left_ref
  408.7 3.5 collective-permute-start.61
  413.6 3.5 collective-permute-start.30
  417.7 2.7 collective-permute-start.62
  422.0 3.8 collective-permute-start.31
  426.0 3.2 collective-permute-done.46.left_ref
  429.6 2.7 collective-permute-start.63
  432.4 2.9 collective-permute-start.32
  437.5 4.9 %collective-permute-done.32 = bf16[128,896]{1,0:T(8,128)(2,1)S(1)} collective-permute-done((bf16[128,896]{1,0:T(8,128)(2,1)S(1)}, bf16[128,896]{1,0:T(8,128)(2,1)S(1)}, u32[]{:S(2)}, u32[]{:S(2)}) %collective-permute-start.32) | collective-permute-done | bytes 229408 | tf_op jit(solution)/shard_map/ppermute | solution.py:207
  444.3 2.2 collective-permute-done.48
  447.8 13.5 %collective-permute-start.64 = (bf16[64,1792]{1,0:T(8,128)(2,1)S(1)}, bf16[64,1792]{1,0:T(8,128)(2,1)S(1)}, u32[]{:S(2)}, u32[]{:S(2)}) collective-permute-start(bf16[64,1792]{1,0:T(8,128)(2,1)S(1)} %dynamic-slice_bitcast_fusion), channel_id=1, source_target_pairs={{0,1},{1,0},{2,3},{3,2},{4,5},{5,4},{6,7},{7,6},{8,9},{9,8},{10,11... | collective-permute-start | bytes 688136 | tf_op jit(solution)/shard_map/ppermute | solution.py:225
  (188 shorter events, 45.7 us)
Async XLA Ops:
  7.1 231.7 %all-to-all-start = ((bf16[64,16,1024]{2,1,0:T(8,128)(2,1)}), bf16[64,16,1024]{2,1,0:T(8,128)(2,1)S(1)}, u32[]{:S(2)}, u32[]{:S(2)}) async-start(bf16[64,16,1024]{2,1,0:T(8,128)(2,1)} %bitcast.45), calls=%async_computation | async-start | bytes 4194304 | tf_op jit(solution)/shard_map/all_to_all | solution.py:171
  41.5 229.8 %collective-permute-start.1 = (bf16[1024,3584]{1,0:T(8,128)(2,1)}, bf16[1024,3584]{1,0:T(8,128)(2,1)}, u32[]{:S(2)}, u32[]{:S(2)}) collective-permute-start(bf16[1024,3584]{1,0:T(8,128)(2,1)} %bitcast.37), channel_id=1, source_target_pairs={{0,1},{1,0},{2,3},{3,2},{4,5},{5,4},{6,7},{7,6},{8,9},{9,8},{10,11... | collective-permute-start | bytes 22020104 | tf_op jit(solution)/shard_map/ppermute | solution.py:159
  238.8 32.4 %collective-permute-start = (bf16[64,16,1024]{2,1,0:T(8,128)(2,1)S(1)}, bf16[64,16,1024]{2,1,0:T(8,128)(2,1)}, u32[]{:S(2)}, u32[]{:S(2)}) collective-permute-start(bf16[64,16,1024]{2,1,0:T(8,128)(2,1)S(1)} %all-to-all-done.refs_1_.refs_2_.refs_3_.refs_4_.refs_5_.refs_6_.refs_7_.refs_8_), channel_id=1, source_target_pairs={{0,1},{1,0},{2,3},{3,2},{4,5},{5,4},{6,7},{7,6},{8,9},{9,8},{10,11... | collective-permute-start | bytes 6291464 | tf_op jit(solution)/shard_map/ppermute | solution.py:174
  241.8 27.5 %all-to-all-start.1 = ((f32[64,1,128]{2,1,0:T(1,128)}), f32[64,1,128]{2,1,0:T(1,128)S(1)}, u32[]{:S(2)}, u32[]{:S(2)}) async-start(f32[64,1,128]{2,1,0:T(1,128)} %bitcast.7), calls=%async_computation.1 | async-start | bytes 65536 | tf_op jit(solution)/shard_map/all_to_all | solution.py:170
  280.7 12.4 %collective-permute-start.33 = (bf16[128,896]{1,0:T(8,128)(2,1)S(1)}, bf16[128,896]{1,0:T(8,128)(2,1)S(1)}, u32[]{:S(2)}, u32[]{:S(2)}) collective-permute-start(bf16[128,896]{1,0:T(8,128)(2,1)S(1)} %get-tuple-element.13), channel_id=1, source_target_pairs={{0,2},{1,3},{2,4},{3,5},{4,6},{5,7},{6,8},{7,9},{8,10},{9,11},{10,... | collective-permute-start | bytes 688136 | tf_op jit(solution)/shard_map/ppermute | solution.py:205
  280.9 12.5 %collective-permute-start.49 = (bf16[128,896]{1,0:T(8,128)(2,1)S(1)}, bf16[128,896]{1,0:T(8,128)(2,1)S(1)}, u32[]{:S(2)}, u32[]{:S(2)}) collective-permute-start(bf16[128,896]{1,0:T(8,128)(2,1)S(1)} %get-tuple-element.12), channel_id=1, source_target_pairs={{0,62},{1,63},{2,0},{3,1},{4,2},{5,3},{6,4},{7,5},{8,6},{9,7},{10,... | collective-permute-start | bytes 688136 | tf_op jit(solution)/shard_map/ppermute | solution.py:207
  283.5 12.7 %collective-permute-start.18 = (bf16[128,896]{1,0:T(8,128)(2,1)S(1)}, bf16[128,896]{1,0:T(8,128)(2,1)S(1)}, u32[]{:S(2)}, u32[]{:S(2)}) collective-permute-start(bf16[128,896]{1,0:T(8,128)(2,1)S(1)} %get-tuple-element.14), channel_id=1, source_target_pairs={{0,62},{1,63},{2,0},{3,1},{4,2},{5,3},{6,4},{7,5},{8,6},{9,7},{10,... | collective-permute-start | bytes 688136 | tf_op jit(solution)/shard_map/ppermute | solution.py:207
  288.3 9.7 %collective-permute-start.3 = (bf16[128,896]{1,0:T(8,128)(2,1)S(1)}, bf16[128,896]{1,0:T(8,128)(2,1)S(1)}, u32[]{:S(2)}, u32[]{:S(2)}) collective-permute-start(bf16[128,896]{1,0:T(8,128)(2,1)S(1)} %shard_map.57), channel_id=1, source_target_pairs={{0,2},{1,3},{2,4},{3,5},{4,6},{5,7},{6,8},{7,9},{8,10},{9,11},{10,... | collective-permute-start | bytes 688136 | tf_op jit(solution)/shard_map/ppermute | solution.py:205
  293.3 9.7 %collective-permute-start.34 = (bf16[128,896]{1,0:T(8,128)(2,1)S(1)}, bf16[128,896]{1,0:T(8,128)(2,1)S(1)}, u32[]{:S(2)}, u32[]{:S(2)}) collective-permute-start(bf16[128,896]{1,0:T(8,128)(2,1)S(1)} %shard_map.89), channel_id=1, source_target_pairs={{0,2},{1,3},{2,4},{3,5},{4,6},{5,7},{6,8},{7,9},{8,10},{9,11},{10,... | collective-permute-start | bytes 688136 | tf_op jit(solution)/shard_map/ppermute | solution.py:205
  293.5 9.7 %collective-permute-start.50 = (bf16[128,896]{1,0:T(8,128)(2,1)S(1)}, bf16[128,896]{1,0:T(8,128)(2,1)S(1)}, u32[]{:S(2)}, u32[]{:S(2)}) collective-permute-start(bf16[128,896]{1,0:T(8,128)(2,1)S(1)} %shard_map.104), channel_id=1, source_target_pairs={{0,62},{1,63},{2,0},{3,1},{4,2},{5,3},{6,4},{7,5},{8,6},{9,7},{10,... | collective-permute-start | bytes 688136 | tf_op jit(solution)/shard_map/ppermute | solution.py:207
  296.4 9.7 %collective-permute-start.19 = (bf16[128,896]{1,0:T(8,128)(2,1)S(1)}, bf16[128,896]{1,0:T(8,128)(2,1)S(1)}, u32[]{:S(2)}, u32[]{:S(2)}) collective-permute-start(bf16[128,896]{1,0:T(8,128)(2,1)S(1)} %shard_map.75), channel_id=1, source_target_pairs={{0,62},{1,63},{2,0},{3,1},{4,2},{5,3},{6,4},{7,5},{8,6},{9,7},{10,... | collective-permute-start | bytes 688136 | tf_op jit(solution)/shard_map/ppermute | solution.py:207
  298.1 9.7 %collective-permute-start.4 = (bf16[128,896]{1,0:T(8,128)(2,1)S(1)}, bf16[128,896]{1,0:T(8,128)(2,1)S(1)}, u32[]{:S(2)}, u32[]{:S(2)}) collective-permute-start(bf16[128,896]{1,0:T(8,128)(2,1)S(1)} %shard_map.58), channel_id=1, source_target_pairs={{0,2},{1,3},{2,4},{3,5},{4,6},{5,7},{6,8},{7,9},{8,10},{9,11},{10,... | collective-permute-start | bytes 688136 | tf_op jit(solution)/shard_map/ppermute | solution.py:205
  303.0 9.7 %collective-permute-start.35 = (bf16[128,896]{1,0:T(8,128)(2,1)S(1)}, bf16[128,896]{1,0:T(8,128)(2,1)S(1)}, u32[]{:S(2)}, u32[]{:S(2)}) collective-permute-start(bf16[128,896]{1,0:T(8,128)(2,1)S(1)} %shard_map.90), channel_id=1, source_target_pairs={{0,2},{1,3},{2,4},{3,5},{4,6},{5,7},{6,8},{7,9},{8,10},{9,11},{10,... | collective-permute-start | bytes 688136 | tf_op jit(solution)/shard_map/ppermute | solution.py:205
  303.3 15.9 %collective-permute-start.51 = (bf16[128,896]{1,0:T(8,128)(2,1)S(1)}, bf16[128,896]{1,0:T(8,128)(2,1)S(1)}, u32[]{:S(2)}, u32[]{:S(2)}) collective-permute-start(bf16[128,896]{1,0:T(8,128)(2,1)S(1)} %shard_map.105), channel_id=1, source_target_pairs={{0,62},{1,63},{2,0},{3,1},{4,2},{5,3},{6,4},{7,5},{8,6},{9,7},{10,... | collective-permute-start | bytes 688136 | tf_op jit(solution)/shard_map/ppermute | solution.py:207
  306.1 15.9 %collective-permute-start.20 = (bf16[128,896]{1,0:T(8,128)(2,1)S(1)}, bf16[128,896]{1,0:T(8,128)(2,1)S(1)}, u32[]{:S(2)}, u32[]{:S(2)}) collective-permute-start(bf16[128,896]{1,0:T(8,128)(2,1)S(1)} %shard_map.76), channel_id=1, source_target_pairs={{0,62},{1,63},{2,0},{3,1},{4,2},{5,3},{6,4},{7,5},{8,6},{9,7},{10,... | collective-permute-start | bytes 688136 | tf_op jit(solution)/shard_map/ppermute | solution.py:207
  307.9 14.4 %collective-permute-start.5 = (bf16[128,896]{1,0:T(8,128)(2,1)S(1)}, bf16[128,896]{1,0:T(8,128)(2,1)S(1)}, u32[]{:S(2)}, u32[]{:S(2)}) collective-permute-start(bf16[128,896]{1,0:T(8,128)(2,1)S(1)} %shard_map.59), channel_id=1, source_target_pairs={{0,2},{1,3},{2,4},{3,5},{4,6},{5,7},{6,8},{7,9},{8,10},{9,11},{10,... | collective-permute-start | bytes 688136 | tf_op jit(solution)/shard_map/ppermute | solution.py:205
  312.8 11.5 %collective-permute-start.36 = (bf16[128,896]{1,0:T(8,128)(2,1)S(1)}, bf16[128,896]{1,0:T(8,128)(2,1)S(1)}, u32[]{:S(2)}, u32[]{:S(2)}) collective-permute-start(bf16[128,896]{1,0:T(8,128)(2,1)S(1)} %shard_map.91), channel_id=1, source_target_pairs={{0,2},{1,3},{2,4},{3,5},{4,6},{5,7},{6,8},{7,9},{8,10},{9,11},{10,... | collective-permute-start | bytes 688136 | tf_op jit(solution)/shard_map/ppermute | solution.py:205
  322.4 9.6 %collective-permute-start.6 = (bf16[128,896]{1,0:T(8,128)(2,1)S(1)}, bf16[128,896]{1,0:T(8,128)(2,1)S(1)}, u32[]{:S(2)}, u32[]{:S(2)}) collective-permute-start(bf16[128,896]{1,0:T(8,128)(2,1)S(1)} %shard_map.61), channel_id=1, source_target_pairs={{0,2},{1,3},{2,4},{3,5},{4,6},{5,7},{6,8},{7,9},{8,10},{9,11},{10,... | collective-permute-start | bytes 688136 | tf_op jit(solution)/shard_map/ppermute | solution.py:205
  329.0 9.7 %collective-permute-start.22 = (bf16[128,896]{1,0:T(8,128)(2,1)S(1)}, bf16[128,896]{1,0:T(8,128)(2,1)S(1)}, u32[]{:S(2)}, u32[]{:S(2)}) collective-permute-start(bf16[128,896]{1,0:T(8,128)(2,1)S(1)} %shard_map.78), channel_id=1, source_target_pairs={{0,62},{1,63},{2,0},{3,1},{4,2},{5,3},{6,4},{7,5},{8,6},{9,7},{10,... | collective-permute-start | bytes 688136 | tf_op jit(solution)/shard_map/ppermute | solution.py:207
  332.1 10.1 %collective-permute-start.7 = (bf16[128,896]{1,0:T(8,128)(2,1)S(1)}, bf16[128,896]{1,0:T(8,128)(2,1)S(1)}, u32[]{:S(2)}, u32[]{:S(2)}) collective-permute-start(bf16[128,896]{1,0:T(8,128)(2,1)S(1)} %shard_map.62), channel_id=1, source_target_pairs={{0,2},{1,3},{2,4},{3,5},{4,6},{5,7},{6,8},{7,9},{8,10},{9,11},{10,... | collective-permute-start | bytes 688136 | tf_op jit(solution)/shard_map/ppermute | solution.py:205
  332.4 10.0 %collective-permute-start.38 = (bf16[128,896]{1,0:T(8,128)(2,1)S(1)}, bf16[128,896]{1,0:T(8,128)(2,1)S(1)}, u32[]{:S(2)}, u32[]{:S(2)}) collective-permute-start(bf16[128,896]{1,0:T(8,128)(2,1)S(1)} %shard_map.93), channel_id=1, source_target_pairs={{0,2},{1,3},{2,4},{3,5},{4,6},{5,7},{6,8},{7,9},{8,10},{9,11},{10,... | collective-permute-start | bytes 688136 | tf_op jit(solution)/shard_map/ppermute | solution.py:205
  334.0 9.7 %collective-permute-start.54 = (bf16[128,896]{1,0:T(8,128)(2,1)S(1)}, bf16[128,896]{1,0:T(8,128)(2,1)S(1)}, u32[]{:S(2)}, u32[]{:S(2)}) collective-permute-start(bf16[128,896]{1,0:T(8,128)(2,1)S(1)} %shard_map.108), channel_id=1, source_target_pairs={{0,62},{1,63},{2,0},{3,1},{4,2},{5,3},{6,4},{7,5},{8,6},{9,7},{10,... | collective-permute-start | bytes 688136 | tf_op jit(solution)/shard_map/ppermute | solution.py:207
  338.9 9.7 %collective-permute-start.23 = (bf16[128,896]{1,0:T(8,128)(2,1)S(1)}, bf16[128,896]{1,0:T(8,128)(2,1)S(1)}, u32[]{:S(2)}, u32[]{:S(2)}) collective-permute-start(bf16[128,896]{1,0:T(8,128)(2,1)S(1)} %shard_map.79), channel_id=1, source_target_pairs={{0,62},{1,63},{2,0},{3,1},{4,2},{5,3},{6,4},{7,5},{8,6},{9,7},{10,... | collective-permute-start | bytes 688136 | tf_op jit(solution)/shard_map/ppermute | solution.py:207
  342.3 9.7 %collective-permute-start.8 = (bf16[128,896]{1,0:T(8,128)(2,1)S(1)}, bf16[128,896]{1,0:T(8,128)(2,1)S(1)}, u32[]{:S(2)}, u32[]{:S(2)}) collective-permute-start(bf16[128,896]{1,0:T(8,128)(2,1)S(1)} %shard_map.63), channel_id=1, source_target_pairs={{0,2},{1,3},{2,4},{3,5},{4,6},{5,7},{6,8},{7,9},{8,10},{9,11},{10,... | collective-permute-start | bytes 688136 | tf_op jit(solution)/shard_map/ppermute | solution.py:205
  342.5 11.8 %collective-permute-start.39 = (bf16[128,896]{1,0:T(8,128)(2,1)S(1)}, bf16[128,896]{1,0:T(8,128)(2,1)S(1)}, u32[]{:S(2)}, u32[]{:S(2)}) collective-permute-start(bf16[128,896]{1,0:T(8,128)(2,1)S(1)} %shard_map.94), channel_id=1, source_target_pairs={{0,2},{1,3},{2,4},{3,5},{4,6},{5,7},{6,8},{7,9},{8,10},{9,11},{10,... | collective-permute-start | bytes 688136 | tf_op jit(solution)/shard_map/ppermute | solution.py:205
  343.8 17.2 %collective-permute-start.55 = (bf16[128,896]{1,0:T(8,128)(2,1)S(1)}, bf16[128,896]{1,0:T(8,128)(2,1)S(1)}, u32[]{:S(2)}, u32[]{:S(2)}) collective-permute-start(bf16[128,896]{1,0:T(8,128)(2,1)S(1)} %shard_map.109), channel_id=1, source_target_pairs={{0,62},{1,63},{2,0},{3,1},{4,2},{5,3},{6,4},{7,5},{8,6},{9,7},{10,... | collective-permute-start | bytes 688136 | tf_op jit(solution)/shard_map/ppermute | solution.py:207
  348.7 15.1 %collective-permute-start.24 = (bf16[128,896]{1,0:T(8,128)(2,1)S(1)}, bf16[128,896]{1,0:T(8,128)(2,1)S(1)}, u32[]{:S(2)}, u32[]{:S(2)}) collective-permute-start(bf16[128,896]{1,0:T(8,128)(2,1)S(1)} %shard_map.80), channel_id=1, source_target_pairs={{0,62},{1,63},{2,0},{3,1},{4,2},{5,3},{6,4},{7,5},{8,6},{9,7},{10,... | collective-permute-start | bytes 688136 | tf_op jit(solution)/shard_map/ppermute | solution.py:207
  352.1 12.0 %collective-permute-start.9 = (bf16[128,896]{1,0:T(8,128)(2,1)S(1)}, bf16[128,896]{1,0:T(8,128)(2,1)S(1)}, u32[]{:S(2)}, u32[]{:S(2)}) collective-permute-start(bf16[128,896]{1,0:T(8,128)(2,1)S(1)} %shard_map.64), channel_id=1, source_target_pairs={{0,2},{1,3},{2,4},{3,5},{4,6},{5,7},{6,8},{7,9},{8,10},{9,11},{10,... | collective-permute-start | bytes 688136 | tf_op jit(solution)/shard_map/ppermute | solution.py:205
  354.4 11.3 %collective-permute-start.40 = (bf16[128,896]{1,0:T(8,128)(2,1)S(1)}, bf16[128,896]{1,0:T(8,128)(2,1)S(1)}, u32[]{:S(2)}, u32[]{:S(2)}) collective-permute-start(bf16[128,896]{1,0:T(8,128)(2,1)S(1)} %shard_map.95), channel_id=1, source_target_pairs={{0,2},{1,3},{2,4},{3,5},{4,6},{5,7},{6,8},{7,9},{8,10},{9,11},{10,... | collective-permute-start | bytes 688136 | tf_op jit(solution)/shard_map/ppermute | solution.py:205
  365.8 9.5 %collective-permute-start.41 = (bf16[128,896]{1,0:T(8,128)(2,1)S(1)}, bf16[128,896]{1,0:T(8,128)(2,1)S(1)}, u32[]{:S(2)}, u32[]{:S(2)}) collective-permute-start(bf16[128,896]{1,0:T(8,128)(2,1)S(1)} %shard_map.96), channel_id=1, source_target_pairs={{0,2},{1,3},{2,4},{3,5},{4,6},{5,7},{6,8},{7,9},{8,10},{9,11},{10,... | collective-permute-start | bytes 688136 | tf_op jit(solution)/shard_map/ppermute | solution.py:205
  375.4 10.6 %collective-permute-start.42 = (bf16[128,896]{1,0:T(8,128)(2,1)S(1)}, bf16[128,896]{1,0:T(8,128)(2,1)S(1)}, u32[]{:S(2)}, u32[]{:S(2)}) collective-permute-start(bf16[128,896]{1,0:T(8,128)(2,1)S(1)} %shard_map.97), channel_id=1, source_target_pairs={{0,2},{1,3},{2,4},{3,5},{4,6},{5,7},{6,8},{7,9},{8,10},{9,11},{10,... | collective-permute-start | bytes 688136 | tf_op jit(solution)/shard_map/ppermute | solution.py:205
  375.7 10.6 %collective-permute-start.58 = (bf16[128,896]{1,0:T(8,128)(2,1)S(1)}, bf16[128,896]{1,0:T(8,128)(2,1)S(1)}, u32[]{:S(2)}, u32[]{:S(2)}) collective-permute-start(bf16[128,896]{1,0:T(8,128)(2,1)S(1)} %shard_map.112), channel_id=1, source_target_pairs={{0,62},{1,63},{2,0},{3,1},{4,2},{5,3},{6,4},{7,5},{8,6},{9,7},{10,... | collective-permute-start | bytes 688136 | tf_op jit(solution)/shard_map/ppermute | solution.py:207
  378.5 10.8 %collective-permute-start.27 = (bf16[128,896]{1,0:T(8,128)(2,1)S(1)}, bf16[128,896]{1,0:T(8,128)(2,1)S(1)}, u32[]{:S(2)}, u32[]{:S(2)}) collective-permute-start(bf16[128,896]{1,0:T(8,128)(2,1)S(1)} %shard_map.83), channel_id=1, source_target_pairs={{0,62},{1,63},{2,0},{3,1},{4,2},{5,3},{6,4},{7,5},{8,6},{9,7},{10,... | collective-permute-start | bytes 688136 | tf_op jit(solution)/shard_map/ppermute | solution.py:207
  381.2 10.2 %collective-permute-start.12 = (bf16[128,896]{1,0:T(8,128)(2,1)S(1)}, bf16[128,896]{1,0:T(8,128)(2,1)S(1)}, u32[]{:S(2)}, u32[]{:S(2)}) collective-permute-start(bf16[128,896]{1,0:T(8,128)(2,1)S(1)} %shard_map.68), channel_id=1, source_target_pairs={{0,2},{1,3},{2,4},{3,5},{4,6},{5,7},{6,8},{7,9},{8,10},{9,11},{10,... | collective-permute-start | bytes 688136 | tf_op jit(solution)/shard_map/ppermute | solution.py:205
  386.3 14.3 %collective-permute-start.59 = (bf16[128,896]{1,0:T(8,128)(2,1)S(1)}, bf16[128,896]{1,0:T(8,128)(2,1)S(1)}, u32[]{:S(2)}, u32[]{:S(2)}) collective-permute-start(bf16[128,896]{1,0:T(8,128)(2,1)S(1)} %shard_map.113), channel_id=1, source_target_pairs={{0,62},{1,63},{2,0},{3,1},{4,2},{5,3},{6,4},{7,5},{8,6},{9,7},{10,... | collective-permute-start | bytes 688136 | tf_op jit(solution)/shard_map/ppermute | solution.py:207
  389.4 14.1 %collective-permute-start.28 = (bf16[128,896]{1,0:T(8,128)(2,1)S(1)}, bf16[128,896]{1,0:T(8,128)(2,1)S(1)}, u32[]{:S(2)}, u32[]{:S(2)}) collective-permute-start(bf16[128,896]{1,0:T(8,128)(2,1)S(1)} %shard_map.84), channel_id=1, source_target_pairs={{0,62},{1,63},{2,0},{3,1},{4,2},{5,3},{6,4},{7,5},{8,6},{9,7},{10,... | collective-permute-start | bytes 688136 | tf_op jit(solution)/shard_map/ppermute | solution.py:207
  391.5 12.3 %collective-permute-start.13 = (bf16[128,896]{1,0:T(8,128)(2,1)S(1)}, bf16[128,896]{1,0:T(8,128)(2,1)S(1)}, u32[]{:S(2)}, u32[]{:S(2)}) collective-permute-start(bf16[128,896]{1,0:T(8,128)(2,1)S(1)} %shard_map.69), channel_id=1, source_target_pairs={{0,2},{1,3},{2,4},{3,5},{4,6},{5,7},{6,8},{7,9},{8,10},{9,11},{10,... | collective-permute-start | bytes 688136 | tf_op jit(solution)/shard_map/ppermute | solution.py:205
  394.3 11.1 %collective-permute-start.44 = (bf16[128,896]{1,0:T(8,128)(2,1)S(1)}, bf16[128,896]{1,0:T(8,128)(2,1)S(1)}, u32[]{:S(2)}, u32[]{:S(2)}) collective-permute-start(bf16[128,896]{1,0:T(8,128)(2,1)S(1)} %shard_map.99), channel_id=1, source_target_pairs={{0,2},{1,3},{2,4},{3,5},{4,6},{5,7},{6,8},{7,9},{8,10},{9,11},{10,... | collective-permute-start | bytes 688136 | tf_op jit(solution)/shard_map/ppermute | solution.py:205
  403.6 9.9 %collective-permute-start.29 = (bf16[128,896]{1,0:T(8,128)(2,1)S(1)}, bf16[128,896]{1,0:T(8,128)(2,1)S(1)}, u32[]{:S(2)}, u32[]{:S(2)}) collective-permute-start(bf16[128,896]{1,0:T(8,128)(2,1)S(1)} %shard_map.85), channel_id=1, source_target_pairs={{0,62},{1,63},{2,0},{3,1},{4,2},{5,3},{6,4},{7,5},{8,6},{9,7},{10,... | collective-permute-start | bytes 688136 | tf_op jit(solution)/shard_map/ppermute | solution.py:207
  403.9 13.2 %collective-permute-start.14 = (bf16[128,896]{1,0:T(8,128)(2,1)S(1)}, bf16[128,896]{1,0:T(8,128)(2,1)S(1)}, u32[]{:S(2)}, u32[]{:S(2)}) collective-permute-start(bf16[128,896]{1,0:T(8,128)(2,1)S(1)} %shard_map.71), channel_id=1, source_target_pairs={{0,2},{1,3},{2,4},{3,5},{4,6},{5,7},{6,8},{7,9},{8,10},{9,11},{10,... | collective-permute-start | bytes 688136 | tf_op jit(solution)/shard_map/ppermute | solution.py:205
  405.5 11.8 %collective-permute-start.45 = (bf16[128,896]{1,0:T(8,128)(2,1)S(1)}, bf16[128,896]{1,0:T(8,128)(2,1)S(1)}, u32[]{:S(2)}, u32[]{:S(2)}) collective-permute-start(bf16[128,896]{1,0:T(8,128)(2,1)S(1)} %shard_map.100), channel_id=1, source_target_pairs={{0,2},{1,3},{2,4},{3,5},{4,6},{5,7},{6,8},{7,9},{8,10},{9,11},{10,... | collective-permute-start | bytes 688136 | tf_op jit(solution)/shard_map/ppermute | solution.py:205
  417.5 11.7 %collective-permute-start.46 = (bf16[128,896]{1,0:T(8,128)(2,1)S(1)}, bf16[128,896]{1,0:T(8,128)(2,1)S(1)}, u32[]{:S(2)}, u32[]{:S(2)}) collective-permute-start(bf16[128,896]{1,0:T(8,128)(2,1)S(1)} %shard_map.101), channel_id=1, source_target_pairs={{0,2},{1,3},{2,4},{3,5},{4,6},{5,7},{6,8},{7,9},{8,10},{9,11},{10,... | collective-permute-start | bytes 688136 | tf_op jit(solution)/shard_map/ppermute | solution.py:205
  417.7 11.7 %collective-permute-start.62 = (bf16[128,896]{1,0:T(8,128)(2,1)S(1)}, bf16[128,896]{1,0:T(8,128)(2,1)S(1)}, u32[]{:S(2)}, u32[]{:S(2)}) collective-permute-start(bf16[128,896]{1,0:T(8,128)(2,1)S(1)} %shard_map.116), channel_id=1, source_target_pairs={{0,62},{1,63},{2,0},{3,1},{4,2},{5,3},{6,4},{7,5},{8,6},{9,7},{10,... | collective-permute-start | bytes 688136 | tf_op jit(solution)/shard_map/ppermute | solution.py:207
  422.0 10.3 %collective-permute-start.31 = (bf16[128,896]{1,0:T(8,128)(2,1)S(1)}, bf16[128,896]{1,0:T(8,128)(2,1)S(1)}, u32[]{:S(2)}, u32[]{:S(2)}) collective-permute-start(bf16[128,896]{1,0:T(8,128)(2,1)S(1)} %shard_map.87), channel_id=1, source_target_pairs={{0,62},{1,63},{2,0},{3,1},{4,2},{5,3},{6,4},{7,5},{8,6},{9,7},{10,... | collective-permute-start | bytes 688136 | tf_op jit(solution)/shard_map/ppermute | solution.py:207
  425.9 9.4 %collective-permute-start.16 = (bf16[128,896]{1,0:T(8,128)(2,1)S(1)}, bf16[128,896]{1,0:T(8,128)(2,1)S(1)}, u32[]{:S(2)}, u32[]{:S(2)}) collective-permute-start(bf16[128,896]{1,0:T(8,128)(2,1)S(1)} %shard_map.73), channel_id=1, source_target_pairs={{0,2},{1,3},{2,4},{3,5},{4,6},{5,7},{6,8},{7,9},{8,10},{9,11},{10,... | collective-permute-start | bytes 688136 | tf_op jit(solution)/shard_map/ppermute | solution.py:205
  432.4 10.0 %collective-permute-start.32 = (bf16[128,896]{1,0:T(8,128)(2,1)S(1)}, bf16[128,896]{1,0:T(8,128)(2,1)S(1)}, u32[]{:S(2)}, u32[]{:S(2)}) collective-permute-start(bf16[128,896]{1,0:T(8,128)(2,1)S(1)} %shard_map.88), channel_id=1, source_target_pairs={{0,62},{1,63},{2,0},{3,1},{4,2},{5,3},{6,4},{7,5},{8,6},{9,7},{10,... | collective-permute-start | bytes 688136 | tf_op jit(solution)/shard_map/ppermute | solution.py:207
  435.8 10.7 %collective-permute-start.48 = (bf16[128,896]{1,0:T(8,128)(2,1)S(1)}, bf16[128,896]{1,0:T(8,128)(2,1)S(1)}, u32[]{:S(2)}, u32[]{:S(2)}) collective-permute-start(bf16[128,896]{1,0:T(8,128)(2,1)S(1)} %shard_map.103), channel_id=1, source_target_pairs={{0,2},{1,3},{2,4},{3,5},{4,6},{5,7},{6,8},{7,9},{8,10},{9,11},{10,... | collective-permute-start | bytes 688136 | tf_op jit(solution)/shard_map/ppermute | solution.py:205
  447.8 14.6 %collective-permute-start.64 = (bf16[64,1792]{1,0:T(8,128)(2,1)S(1)}, bf16[64,1792]{1,0:T(8,128)(2,1)S(1)}, u32[]{:S(2)}, u32[]{:S(2)}) collective-permute-start(bf16[64,1792]{1,0:T(8,128)(2,1)S(1)} %dynamic-slice_bitcast_fusion), channel_id=1, source_target_pairs={{0,1},{1,0},{2,3},{3,2},{4,5},{5,4},{6,7},{7,6},{8,9},{9,8},{10,11... | collective-permute-start | bytes 688136 | tf_op jit(solution)/shard_map/ppermute | solution.py:225
  (25 other events, 205.0 us)

commit v2 on v1

v2 whole, which is shorter than its diff:
```python
import jax
import jax.numpy as jnp
from jax import lax
from jax.experimental import pallas as pl
from jax.experimental.pallas import tpu as pltpu
from jax.sharding import PartitionSpec as P

CHAINS = 2
BATCH = 4
INTERPRET = False


def strictly_before(size):
    earlier = lax.broadcasted_iota(jnp.int32, (size, size), 0)
    return (earlier < lax.broadcasted_iota(jnp.int32, (size, size), 1)).astype(jnp.bfloat16)


def pack_kernel(target_ref, routed_ref, rows_ref, *, experts, capacity):
    pairs, width = routed_ref.shape
    half = width // 2
    target = target_ref[...]
    named = lax.broadcasted_iota(jnp.int32, (experts, pairs), 0) == target
    earlier = jnp.dot(
        named.astype(jnp.bfloat16), strictly_before(pairs), preferred_element_type=jnp.float32
    )
    rank = jnp.sum(jnp.where(named, earlier, 0.0), axis=0, keepdims=True).astype(jnp.int32)
    slot = target * capacity + rank
    gate = routed_ref[:, :half].astype(jnp.float32)
    upper = routed_ref[:, half:].astype(jnp.float32)
    hidden = (gate / (1.0 + jnp.exp(-gate)) * upper).astype(jnp.bfloat16)
    pick = (
        lax.broadcasted_iota(jnp.int32, (experts * capacity, pairs), 0) == slot
    ).astype(jnp.bfloat16)
    rows_ref[...] = jnp.dot(pick, hidden, preferred_element_type=jnp.float32).astype(jnp.bfloat16)


def table_kernel(place_ref, routes_ref, token_ref, gate_ref, *, capacity, chosen):
    pairs = routes_ref.shape[1] // 2
    target = routes_ref[:, :pairs]
    gates = routes_ref[:, pairs:]
    before = strictly_before(pairs)
    number = (lax.broadcasted_iota(jnp.int32, target.shape, 1) // chosen).astype(jnp.float32)
    lane = lax.broadcasted_iota(jnp.int32, token_ref.shape, 1)
    period = 2 * capacity
    token = jnp.zeros(token_ref.shape, jnp.float32)
    gate = jnp.zeros(token_ref.shape, jnp.float32)
    own = place_ref[2]
    for side in range(2):
        expert = own + side * (1 - 2 * lax.rem(own, 2))
        named = target == expert.astype(jnp.float32)
        rank = jnp.dot(named.astype(jnp.bfloat16), before, preferred_element_type=jnp.float32)
        for k in range(capacity):
            found = jnp.where(named & (rank == k), 1.0, 0.0)
            here = lane % period == side * capacity + k
            token = jnp.where(here, jnp.sum(found * number, axis=1, keepdims=True), token)
            gate = jnp.where(here, jnp.sum(found * gates, axis=1, keepdims=True), gate)
    high = gate.astype(jnp.bfloat16).astype(jnp.float32)
    rest = gate - high
    middle = rest.astype(jnp.bfloat16).astype(jnp.float32)
    token_ref[...] = token
    gate_ref[...] = jnp.where(
        lane < period, high, jnp.where(lane < 2 * period, middle, rest - middle)
    )


def expert_kernel(place_ref, *refs, count):
    own_rows, other_rows = refs[:count], refs[count : 2 * count]
    own_weight, other_weight, token_ref, gate_ref, out_ref = refs[2 * count :]
    capacity = own_rows[0].shape[1]
    tokens = out_ref.shape[1]

    def project(blocks, weight):
        rows = jnp.concatenate([b[0] for b in blocks], axis=0)
        return jnp.dot(rows, weight[...], preferred_element_type=jnp.float32).astype(jnp.bfloat16)

    own = project(own_rows, own_weight)
    other = project(other_rows, other_weight)
    lanes = 6 * capacity
    wanted = lax.broadcasted_iota(jnp.int32, (tokens, lanes), 0).astype(jnp.float32)
    for i in range(count):
        at = slice(i * capacity, (i + 1) * capacity)
        stacked = jnp.concatenate([own[at], other[at]] * 3, axis=0)
        scale = jnp.where(
            token_ref[i : i + 1, :lanes] == wanted, gate_ref[i : i + 1, :lanes], 0.0
        ).astype(jnp.bfloat16)
        out_ref[i] = jnp.dot(scale, stacked, preferred_element_type=jnp.float32).astype(
            jnp.bfloat16
        )


def expert_call(place, rows, own_weight, other_weight, token, gate, homes, tokens):
    chips, both, width = rows.shape
    capacity = both // 2
    columns = own_weight.shape[1]
    piece = columns // 4
    count = len(homes)

    def row_spec(home, side):
        return pl.BlockSpec(
            (1, capacity, width),
            lambda j, s: (lax.rem(s[0] + (home + chips), chips), lax.rem(s[1] + side, 2), 0),
        )

    weight_spec = pl.BlockSpec((width, piece), lambda j, s: (0, j))
    table_spec = pl.BlockSpec(token.shape, lambda j, s: (0, 0))
    grid_spec = pltpu.PrefetchScalarGridSpec(
        num_scalar_prefetch=1,
        grid=(columns // piece,),
        in_specs=[row_spec(h, 0) for h in homes]
        + [row_spec(h, 1) for h in homes]
        + [weight_spec] * 2
        + [table_spec] * 2,
        out_specs=pl.BlockSpec((count, tokens, piece), lambda j, s: (0, 0, j)),
    )
    return pl.pallas_call(
        lambda *refs: expert_kernel(*refs, count=count),
        grid_spec=grid_spec,
        out_shape=jax.ShapeDtypeStruct((count, tokens, columns), jnp.bfloat16),
        compiler_params=pltpu.CompilerParams(
            dimension_semantics=("arbitrary",), vmem_limit_bytes=32 * 1024 * 1024
        ),
        interpret=INTERPRET,
    )(place, *([rows] * (2 * count)), own_weight, other_weight, token, gate)


def add_kernel(left_ref, right_ref, out_ref):
    def some(i, carry):
        at = pl.ds(pl.multiple_of(i * 16, 16), 16)
        total = left_ref[at].astype(jnp.float32) + right_ref[0, at].astype(jnp.float32)
        out_ref[at] = total.astype(jnp.bfloat16)
        return carry

    lax.fori_loop(0, out_ref.shape[0] // 16, some, 0)


def add_own(arrived, batch, place, chain):
    return pl.pallas_call(
        add_kernel,
        grid=(1,),
        in_specs=[
            pl.BlockSpec(arrived.shape, lambda i: (0, 0)),
            pl.BlockSpec((1,) + arrived.shape, lambda i: (place, chain, 0)),
        ],
        out_specs=pl.BlockSpec(arrived.shape, lambda i: (0, 0)),
        out_shape=jax.ShapeDtypeStruct(arrived.shape, jnp.bfloat16),
        compiler_params=pltpu.CompilerParams(vmem_limit_bytes=4 * 1024 * 1024),
        interpret=INTERPRET,
    )(arrived, batch)


def on_device(expert_ids, route_gates, routed_in, down_weight, slot_offset):
    experts = lax.axis_size("ep")
    chips = experts // 2
    tokens, chosen = expert_ids.shape
    pairs = tokens * chosen
    capacity = 2 * pairs // experts
    hidden_width = routed_in.shape[2] // 2
    weight = down_weight[0]
    index = lax.axis_index("ep")
    place = jnp.stack([index // 2, lax.rem(index, 2), index]).astype(jnp.int32)

    def shifted(value, distance):
        return lax.ppermute(
            value, "ep", [(i, (i + 2 * distance) % experts) for i in range(experts)]
        )

    target = jnp.mod(expert_ids - slot_offset[0], experts).reshape(1, pairs)
    rows = pl.pallas_call(
        lambda *refs: pack_kernel(*refs, experts=experts, capacity=capacity),
        out_shape=jax.ShapeDtypeStruct((experts * capacity, hidden_width), jnp.bfloat16),
        compiler_params=pltpu.CompilerParams(vmem_limit_bytes=32 * 1024 * 1024),
        interpret=INTERPRET,
    )(target, routed_in.reshape(pairs, 2 * hidden_width))
    same_core = [[2 * z + c for z in range(chips)] for c in range(2)]
    rows = lax.all_to_all(
        rows.reshape(chips, 2 * capacity, hidden_width),
        "ep",
        split_axis=0,
        concat_axis=0,
        axis_index_groups=same_core,
        tiled=True,
    )
    routes = jnp.concatenate([target.astype(jnp.float32), route_gates.reshape(1, pairs)], axis=1)
    origin = [0]
    distance, sign = chips // 2, 1
    while distance:
        routes = jnp.concatenate([routes, shifted(routes, sign * distance)], axis=0)
        origin = origin + [o - sign * distance for o in origin]
        distance, sign = distance // 2, -sign
    other_weight = lax.ppermute(weight, "ep", [(i, i ^ 1) for i in range(experts)])

    half = chips // 2
    batches = []
    for first in range(0, half, BATCH):
        steps = range(first, first + BATCH)
        batches.append([half - s for s in steps] + [s + 1 - half for s in steps])
    order = [origin.index(next(o for o in origin if (o - h) % chips == 0)) for b in batches for h in b]
    routes = jnp.concatenate([routes[o : o + 1] for o in order], axis=0)
    table = jax.ShapeDtypeStruct((chips, 8 * capacity), jnp.float32)
    token, gate = pl.pallas_call(
        lambda *refs: table_kernel(*refs, capacity=capacity, chosen=chosen),
        in_specs=[
            pl.BlockSpec(memory_space=pltpu.SMEM),
            pl.BlockSpec(memory_space=pltpu.VMEM),
        ],
        out_shape=(table, table),
        compiler_params=pltpu.CompilerParams(vmem_limit_bytes=8 * 1024 * 1024),
        interpret=INTERPRET,
    )(place, routes)

    sums = {}
    for n, homes in enumerate(batches):
        part = slice(n * 2 * BATCH, (n + 1) * 2 * BATCH)
        out = expert_call(
            place, rows, weight, other_weight, token[part], gate[part], homes, tokens
        )
        for i, home in enumerate(homes):
            sums[home] = (out, i)
    share = tokens // CHAINS

    def own_sum(home, c):
        batch, i = sums[home]
        return batch[i, c * share : (c + 1) * share]

    def with_own(arrived, home, c):
        batch, i = sums[home]
        return add_own(arrived, batch, i, c)

    ahead = [own_sum(half, c) for c in range(CHAINS)]
    behind = [own_sum(1 - half, c) for c in range(CHAINS)]
    for step in range(half):
        for c in range(CHAINS):
            ahead[c] = shifted(ahead[c], 1)
            if step < half - 1:
                behind[c] = shifted(behind[c], -1)
                ahead[c] = with_own(ahead[c], half - 1 - step, c)
            if step < half - 2:
                behind[c] = with_own(behind[c], step + 2 - half, c)
    return jnp.concatenate(
        [
            (
                ahead[c].astype(jnp.float32)
                + behind[c].astype(jnp.float32)
                + own_sum(0, c).astype(jnp.float32)
            ).astype(jnp.bfloat16)
            for c in range(CHAINS)
        ],
        axis=0,
    )


def solution(mesh):
    placed = (
        P(("grp", "ep"), None),
        P(("grp", "ep"), None),
        P(("grp", "ep"), None, None),
        P("ep", None, None),
        P(),
    )
    return jax.shard_map(
        on_device, mesh=mesh, in_specs=placed, out_specs=P(("grp", "ep"), None), check_vma=False
    )
```

time: 473 us -> 465 us (0.983)
  the two profiles are of different devices: /device:TPU:37 before, /device:TPU:44 now
where the time goes in v2:
time: 465 us; the launch traced here: 456 us
  waiting for transfers between devices  246 us (53%)
  starting transfers between devices  163 us (35%)
  Pallas kernels  36.4 us (8%)
  local copies, waits for them, and re-layouts  6.86 us (1%)
    ppermute x67, waiting for transfers between devices, shifted(): lax.ppermute(value, 'ep', [(i, (i + 2 * distance) % experts) for i in ran...  246 us
    ppermute x67, starting transfers between devices, shifted(): lax.ppermute(value, 'ep', [(i, (i + 2 * distance) % experts) for i in ran...  130 us
    all_to_all x1, starting transfers between devices, on_device(): lax.all_to_all(rows.reshape(chips, 2 * capacity, hidden_width), 'ep', spl...  32.7 us
    pallas_call x4, Pallas kernels, expert_call(): pl.pallas_call(lambda *refs: expert_kernel(*refs, count=count), grid_spec...  30 us
  transfers between devices with their start and end apart: 69, of which 30 were waited for; matrix products, arithmetic and copies ran while one was open for 0% of the time, Pallas kernels for 6%

profile of v2, /device:TPU:44, one launch (start us, length us, event | category | flops | bytes accessed | tf_op | source)
XLA Modules:
  0.0 456.0 jit_solution(1224568444168572856)
XLA Ops:
  6.1 32.7 %all-to-all-start = ((bf16[32,32,1024]{2,1,0:T(8,128)(2,1)}), bf16[32,32,1024]{2,1,0:T(8,128)(2,1)S(1)}, u32[]{:S(2)}, u32[]{:S(2)}) async-start(bf16[32,32,1024]{2,1,0:T(8,128)(2,1)} %bitcast.33), calls=%async_computation | async-start | bytes 4194304 | tf_op jit(solution)/shard_map/all_to_all | solution.py:175
  39.1 19.8 %collective-permute-start.1 = (f32[1,1024]{1,0:T(1,128)S(1)}, f32[1,1024]{1,0:T(1,128)S(1)}, u32[]{:S(2)}, u32[]{:S(2)}) collective-permute-start(f32[1,1024]{1,0:T(1,128)S(1)} %pad_maximum_fusion.4), channel_id=1, source_target_pairs={{0,32},{1,33},{2,34},{3,35},{4,36},{5,37},{6,38},{7,39},{8,40},{9,... | collective-permute-start | bytes 12296 | tf_op jit(solution)/shard_map/ppermute | solution.py:163
  58.9 171.5 %collective-permute-done.1 = f32[1,1024]{1,0:T(1,128)S(1)} collective-permute-done((f32[1,1024]{1,0:T(1,128)S(1)}, f32[1,1024]{1,0:T(1,128)S(1)}, u32[]{:S(2)}, u32[]{:S(2)}) %collective-permute-start.1) | collective-permute-done | bytes 4128 | tf_op jit(solution)/shard_map/ppermute | solution.py:163
  230.4 8.3 %collective-permute-start.2 = (f32[2,1024]{1,0:T(2,128)S(1)}, f32[2,1024]{1,0:T(2,128)S(1)}, u32[]{:S(2)}, u32[]{:S(2)}) collective-permute-start(f32[2,1024]{1,0:T(2,128)S(1)} %pad_maximum_fusion.3), channel_id=1, source_target_pairs={{0,48},{1,49},{2,50},{3,51},{4,52},{5,53},{6,54},{7,55},{8,56},{9,... | collective-permute-start | bytes 24584 | tf_op jit(solution)/shard_map/ppermute | solution.py:163
  238.8 4.1 collective-permute-done.2
  242.9 3.6 collective-permute-start.3
  246.6 7.4 %collective-permute-done.3 = f32[4,1024]{1,0:T(4,128)S(1)} collective-permute-done((f32[4,1024]{1,0:T(4,128)S(1)}, f32[4,1024]{1,0:T(4,128)S(1)}, u32[]{:S(2)}, u32[]{:S(2)}) %collective-permute-start.3) | collective-permute-done | bytes 16416 | tf_op jit(solution)/shard_map/ppermute | solution.py:163
  254.0 2.6 collective-permute-start.4
  256.6 2.6 collective-permute-done.4
  259.9 4.9 %collective-permute-done.5 = f32[16,1024]{1,0:T(8,128)S(1)} collective-permute-done((f32[16,1024]{1,0:T(8,128)S(1)}, f32[16,1024]{1,0:T(8,128)S(1)}, u32[]{:S(2)}, u32[]{:S(2)}) %collective-permute-start.5) | collective-permute-done | bytes 65568 | tf_op jit(solution)/shard_map/ppermute | solution.py:163
  266.5 3.1 copy-done
  269.5 7.5 %shard_map.57.right_ref = bf16[8,64,3584]{2,1,0:T(8,128)(2,1)S(1)} custom-call(s32[3]{0:T(128)S(1)} %pad_add_fusion.refs_0_, bf16[32,32,1024]{2,1,0:T(8,128)(2,1)S(1)} %all-to-all-done.refs_1_.refs_2_.refs_3_.refs_4_.refs_5_.refs_6_.refs_7_.refs_8_.refs_9_.refs_10_.refs_11_.refs_12_.refs_13_.refs_14_.refs_15_.refs_16_, ...), custom_call_target="tpu_custom_call" | custom-call | tf_op jit(solution)/shard_map/pallas_call | solution.py:115
  278.1 2.5 collective-permute-start.53
  282.7 4.2 collective-permute-done.6.left_ref
  287.1 4.7 %collective-permute-done.37.left_ref = bf16[32,3584]{1,0:T(8,128)(2,1)S(1)} collective-permute-done((bf16[32,3584]{1,0:T(8,128)(2,1)S(1)}, bf16[32,3584]{1,0:T(8,128)(2,1)S(1)}, u32[]{:S(2)}, u32[]{:S(2)}) %collective-permute-start.37) | collective-permute-done | bytes 229408 | tf_op jit(solution)/shard_map/ppermute | solution.py:163
  292.1 3.3 collective-permute-start.54
  297.8 3.9 collective-permute-done.38.left_ref
  302.0 3.3 collective-permute-start.55
  305.4 3.6 collective-permute-start.24
  309.2 2.3 collective-permute-done.39.left_ref
  311.7 7.5 %shard_map.61.right_ref = bf16[8,64,3584]{2,1,0:T(8,128)(2,1)S(1)} custom-call(s32[3]{0:T(128)S(1)} %pad_add_fusion.refs_0_, bf16[32,32,1024]{2,1,0:T(8,128)(2,1)S(1)} %all-to-all-done.refs_1_.refs_2_.refs_3_.refs_4_.refs_5_.refs_6_.refs_7_.refs_8_.refs_9_.refs_10_.refs_11_.refs_12_.refs_13_.refs_14_.refs_15_.refs_16_, ...), custom_call_target="tpu_custom_call" | custom-call | tf_op jit(solution)/shard_map/pallas_call | solution.py:115
  319.3 3.3 collective-permute-start.56
  322.9 2.5 collective-permute-start.10
  326.3 3.8 collective-permute-start.57
  331.0 3.2 collective-permute-start.26
  334.4 3.6 collective-permute-done.41.left_ref
  338.3 3.3 collective-permute-start.58
  341.6 3.2 collective-permute-start.27
  347.4 3.3 collective-permute-start.59
  355.4 7.5 %shard_map.66.right_ref = bf16[8,64,3584]{2,1,0:T(8,128)(2,1)S(1)} custom-call(s32[3]{0:T(128)S(1)} %pad_add_fusion.refs_0_, bf16[32,32,1024]{2,1,0:T(8,128)(2,1)S(1)} %all-to-all-done.refs_1_.refs_2_.refs_3_.refs_4_.refs_5_.refs_6_.refs_7_.refs_8_.refs_9_.refs_10_.refs_11_.refs_12_.refs_13_.refs_14_.refs_15_.refs_16_, ...), custom_call_target="tpu_custom_call" | custom-call | tf_op jit(solution)/shard_map/pallas_call | solution.py:115
  363.0 3.5 collective-permute-start.60
  369.1 3.1 collective-permute-done.60.left_ref
  372.3 3.8 collective-permute-start.61
  377.2 3.8 collective-permute-start.30
  381.8 3.3 collective-permute-start.62
  387.1 3.8 collective-permute-start.31
  391.1 4.3 collective-permute-done.46.left_ref
  395.6 3.3 collective-permute-start.63
  401.3 3.9 collective-permute-done.47.left_ref
  405.6 7.5 %shard_map.71.right_ref = bf16[8,64,3584]{2,1,0:T(8,128)(2,1)S(1)} custom-call(s32[3]{0:T(128)S(1)} %pad_add_fusion.refs_0_, bf16[32,32,1024]{2,1,0:T(8,128)(2,1)S(1)} %all-to-all-done.refs_1_.refs_2_.refs_3_.refs_4_.refs_5_.refs_6_.refs_7_.refs_8_.refs_9_.refs_10_.refs_11_.refs_12_.refs_13_.refs_14_.refs_15_.refs_16_, ...), custom_call_target="tpu_custom_call" | custom-call | tf_op jit(solution)/shard_map/pallas_call | solution.py:115
  413.2 3.3 collective-permute-start.64
  420.5 3.8 collective-permute-start.65
  425.4 3.8 collective-permute-start.34
  431.5 3.3 collective-permute-start.66
  439.4 3.6 collective-permute-start.67
  446.7 2.4 collective-permute-done.36
  449.2 3.0 collective-permute-done.21
  452.1 2.5 collective-permute-done.52
  (188 shorter events, 51.0 us)
Async XLA Ops:
  6.1 260.3 %all-to-all-start = ((bf16[32,32,1024]{2,1,0:T(8,128)(2,1)}), bf16[32,32,1024]{2,1,0:T(8,128)(2,1)S(1)}, u32[]{:S(2)}, u32[]{:S(2)}) async-start(bf16[32,32,1024]{2,1,0:T(8,128)(2,1)} %bitcast.33), calls=%async_computation | async-start | bytes 4194304 | tf_op jit(solution)/shard_map/all_to_all | solution.py:175
  38.8 227.7 %collective-permute-start = (bf16[1024,3584]{1,0:T(8,128)(2,1)}, bf16[1024,3584]{1,0:T(8,128)(2,1)}, u32[]{:S(2)}, u32[]{:S(2)}) collective-permute-start(bf16[1024,3584]{1,0:T(8,128)(2,1)} %bitcast.26), channel_id=1, source_target_pairs={{0,1},{1,0},{2,3},{3,2},{4,5},{5,4},{6,7},{7,6},{8,9},{9,8},{10,11... | collective-permute-start | bytes 22020104 | tf_op jit(solution)/shard_map/ppermute | solution.py:190
  39.1 191.3 %collective-permute-start.1 = (f32[1,1024]{1,0:T(1,128)S(1)}, f32[1,1024]{1,0:T(1,128)S(1)}, u32[]{:S(2)}, u32[]{:S(2)}) collective-permute-start(f32[1,1024]{1,0:T(1,128)S(1)} %pad_maximum_fusion.4), channel_id=1, source_target_pairs={{0,32},{1,33},{2,34},{3,35},{4,36},{5,37},{6,38},{7,39},{8,40},{9,... | collective-permute-start | bytes 12296 | tf_op jit(solution)/shard_map/ppermute | solution.py:163
  230.4 12.5 %collective-permute-start.2 = (f32[2,1024]{1,0:T(2,128)S(1)}, f32[2,1024]{1,0:T(2,128)S(1)}, u32[]{:S(2)}, u32[]{:S(2)}) collective-permute-start(f32[2,1024]{1,0:T(2,128)S(1)} %pad_maximum_fusion.3), channel_id=1, source_target_pairs={{0,48},{1,49},{2,50},{3,51},{4,52},{5,53},{6,54},{7,55},{8,56},{9,... | collective-permute-start | bytes 24584 | tf_op jit(solution)/shard_map/ppermute | solution.py:163
  242.9 11.0 %collective-permute-start.3 = (f32[4,1024]{1,0:T(4,128)S(1)}, f32[4,1024]{1,0:T(4,128)S(1)}, u32[]{:S(2)}, u32[]{:S(2)}) collective-permute-start(f32[4,1024]{1,0:T(4,128)S(1)} %pad_maximum_fusion.2), channel_id=1, source_target_pairs={{0,8},{1,9},{2,10},{3,11},{4,12},{5,13},{6,14},{7,15},{8,16},{9,17... | collective-permute-start | bytes 49160 | tf_op jit(solution)/shard_map/ppermute | solution.py:163
  277.1 9.8 %collective-permute-start.6 = (bf16[32,3584]{1,0:T(8,128)(2,1)S(1)}, bf16[32,3584]{1,0:T(8,128)(2,1)S(1)}, u32[]{:S(2)}, u32[]{:S(2)}) collective-permute-start(bf16[32,3584]{1,0:T(8,128)(2,1)S(1)} %get-tuple-element.11), channel_id=1, source_target_pairs={{0,2},{1,3},{2,4},{3,5},{4,6},{5,7},{6,8},{7,9},{8,10},{9,11},{10,... | collective-permute-start | bytes 688136 | tf_op jit(solution)/shard_map/ppermute | solution.py:163
  277.3 14.6 %collective-permute-start.37 = (bf16[32,3584]{1,0:T(8,128)(2,1)S(1)}, bf16[32,3584]{1,0:T(8,128)(2,1)S(1)}, u32[]{:S(2)}, u32[]{:S(2)}) collective-permute-start(bf16[32,3584]{1,0:T(8,128)(2,1)S(1)} %get-tuple-element.13), channel_id=1, source_target_pairs={{0,2},{1,3},{2,4},{3,5},{4,6},{5,7},{6,8},{7,9},{8,10},{9,11},{10,... | collective-permute-start | bytes 688136 | tf_op jit(solution)/shard_map/ppermute | solution.py:163
  278.1 13.9 %collective-permute-start.53 = (bf16[32,3584]{1,0:T(8,128)(2,1)S(1)}, bf16[32,3584]{1,0:T(8,128)(2,1)S(1)}, u32[]{:S(2)}, u32[]{:S(2)}) collective-permute-start(bf16[32,3584]{1,0:T(8,128)(2,1)S(1)} %get-tuple-element.12), channel_id=1, source_target_pairs={{0,62},{1,63},{2,0},{3,1},{4,2},{5,3},{6,4},{7,5},{8,6},{9,7},{10,... | collective-permute-start | bytes 688136 | tf_op jit(solution)/shard_map/ppermute | solution.py:163
  280.6 14.8 %collective-permute-start.22 = (bf16[32,3584]{1,0:T(8,128)(2,1)S(1)}, bf16[32,3584]{1,0:T(8,128)(2,1)S(1)}, u32[]{:S(2)}, u32[]{:S(2)}) collective-permute-start(bf16[32,3584]{1,0:T(8,128)(2,1)S(1)} %get-tuple-element.14), channel_id=1, source_target_pairs={{0,62},{1,63},{2,0},{3,1},{4,2},{5,3},{6,4},{7,5},{8,6},{9,7},{10,... | collective-permute-start | bytes 688136 | tf_op jit(solution)/shard_map/ppermute | solution.py:163
  287.0 9.8 %collective-permute-start.7 = (bf16[32,3584]{1,0:T(8,128)(2,1)S(1)}, bf16[32,3584]{1,0:T(8,128)(2,1)S(1)}, u32[]{:S(2)}, u32[]{:S(2)}) collective-permute-start(bf16[32,3584]{1,0:T(8,128)(2,1)S(1)} %shard_map.58), channel_id=1, source_target_pairs={{0,2},{1,3},{2,4},{3,5},{4,6},{5,7},{6,8},{7,9},{8,10},{9,11},{10,... | collective-permute-start | bytes 688136 | tf_op jit(solution)/shard_map/ppermute | solution.py:163
  291.9 9.8 %collective-permute-start.38 = (bf16[32,3584]{1,0:T(8,128)(2,1)S(1)}, bf16[32,3584]{1,0:T(8,128)(2,1)S(1)}, u32[]{:S(2)}, u32[]{:S(2)}) collective-permute-start(bf16[32,3584]{1,0:T(8,128)(2,1)S(1)} %shard_map.90), channel_id=1, source_target_pairs={{0,2},{1,3},{2,4},{3,5},{4,6},{5,7},{6,8},{7,9},{8,10},{9,11},{10,... | collective-permute-start | bytes 688136 | tf_op jit(solution)/shard_map/ppermute | solution.py:163
  292.1 9.8 %collective-permute-start.54 = (bf16[32,3584]{1,0:T(8,128)(2,1)S(1)}, bf16[32,3584]{1,0:T(8,128)(2,1)S(1)}, u32[]{:S(2)}, u32[]{:S(2)}) collective-permute-start(bf16[32,3584]{1,0:T(8,128)(2,1)S(1)} %shard_map.105), channel_id=1, source_target_pairs={{0,62},{1,63},{2,0},{3,1},{4,2},{5,3},{6,4},{7,5},{8,6},{9,7},{10,... | collective-permute-start | bytes 688136 | tf_op jit(solution)/shard_map/ppermute | solution.py:163
  295.5 9.8 %collective-permute-start.23 = (bf16[32,3584]{1,0:T(8,128)(2,1)S(1)}, bf16[32,3584]{1,0:T(8,128)(2,1)S(1)}, u32[]{:S(2)}, u32[]{:S(2)}) collective-permute-start(bf16[32,3584]{1,0:T(8,128)(2,1)S(1)} %shard_map.76), channel_id=1, source_target_pairs={{0,62},{1,63},{2,0},{3,1},{4,2},{5,3},{6,4},{7,5},{8,6},{9,7},{10,... | collective-permute-start | bytes 688136 | tf_op jit(solution)/shard_map/ppermute | solution.py:163
  296.8 12.1 %collective-permute-start.8 = (bf16[32,3584]{1,0:T(8,128)(2,1)S(1)}, bf16[32,3584]{1,0:T(8,128)(2,1)S(1)}, u32[]{:S(2)}, u32[]{:S(2)}) collective-permute-start(bf16[32,3584]{1,0:T(8,128)(2,1)S(1)} %shard_map.59), channel_id=1, source_target_pairs={{0,2},{1,3},{2,4},{3,5},{4,6},{5,7},{6,8},{7,9},{8,10},{9,11},{10,... | collective-permute-start | bytes 688136 | tf_op jit(solution)/shard_map/ppermute | solution.py:163
  301.8 9.7 %collective-permute-start.39 = (bf16[32,3584]{1,0:T(8,128)(2,1)S(1)}, bf16[32,3584]{1,0:T(8,128)(2,1)S(1)}, u32[]{:S(2)}, u32[]{:S(2)}) collective-permute-start(bf16[32,3584]{1,0:T(8,128)(2,1)S(1)} %shard_map.91), channel_id=1, source_target_pairs={{0,2},{1,3},{2,4},{3,5},{4,6},{5,7},{6,8},{7,9},{8,10},{9,11},{10,... | collective-permute-start | bytes 688136 | tf_op jit(solution)/shard_map/ppermute | solution.py:163
  302.0 17.2 %collective-permute-start.55 = (bf16[32,3584]{1,0:T(8,128)(2,1)S(1)}, bf16[32,3584]{1,0:T(8,128)(2,1)S(1)}, u32[]{:S(2)}, u32[]{:S(2)}) collective-permute-start(bf16[32,3584]{1,0:T(8,128)(2,1)S(1)} %shard_map.106), channel_id=1, source_target_pairs={{0,62},{1,63},{2,0},{3,1},{4,2},{5,3},{6,4},{7,5},{8,6},{9,7},{10,... | collective-permute-start | bytes 688136 | tf_op jit(solution)/shard_map/ppermute | solution.py:163
  305.4 17.2 %collective-permute-start.24 = (bf16[32,3584]{1,0:T(8,128)(2,1)S(1)}, bf16[32,3584]{1,0:T(8,128)(2,1)S(1)}, u32[]{:S(2)}, u32[]{:S(2)}) collective-permute-start(bf16[32,3584]{1,0:T(8,128)(2,1)S(1)} %shard_map.77), channel_id=1, source_target_pairs={{0,62},{1,63},{2,0},{3,1},{4,2},{5,3},{6,4},{7,5},{8,6},{9,7},{10,... | collective-permute-start | bytes 688136 | tf_op jit(solution)/shard_map/ppermute | solution.py:163
  309.0 13.8 %collective-permute-start.9 = (bf16[32,3584]{1,0:T(8,128)(2,1)S(1)}, bf16[32,3584]{1,0:T(8,128)(2,1)S(1)}, u32[]{:S(2)}, u32[]{:S(2)}) collective-permute-start(bf16[32,3584]{1,0:T(8,128)(2,1)S(1)} %shard_map.60), channel_id=1, source_target_pairs={{0,2},{1,3},{2,4},{3,5},{4,6},{5,7},{6,8},{7,9},{8,10},{9,11},{10,... | collective-permute-start | bytes 688136 | tf_op jit(solution)/shard_map/ppermute | solution.py:163
  311.5 13.9 %collective-permute-start.40 = (bf16[32,3584]{1,0:T(8,128)(2,1)S(1)}, bf16[32,3584]{1,0:T(8,128)(2,1)S(1)}, u32[]{:S(2)}, u32[]{:S(2)}) collective-permute-start(bf16[32,3584]{1,0:T(8,128)(2,1)S(1)} %shard_map.92), channel_id=1, source_target_pairs={{0,2},{1,3},{2,4},{3,5},{4,6},{5,7},{6,8},{7,9},{8,10},{9,11},{10,... | collective-permute-start | bytes 688136 | tf_op jit(solution)/shard_map/ppermute | solution.py:163
  322.9 11.3 %collective-permute-start.10 = (bf16[32,3584]{1,0:T(8,128)(2,1)S(1)}, bf16[32,3584]{1,0:T(8,128)(2,1)S(1)}, u32[]{:S(2)}, u32[]{:S(2)}) collective-permute-start(bf16[32,3584]{1,0:T(8,128)(2,1)S(1)} %shard_map.62), channel_id=1, source_target_pairs={{0,2},{1,3},{2,4},{3,5},{4,6},{5,7},{6,8},{7,9},{8,10},{9,11},{10,... | collective-permute-start | bytes 688136 | tf_op jit(solution)/shard_map/ppermute | solution.py:163
  325.4 12.5 %collective-permute-start.41 = (bf16[32,3584]{1,0:T(8,128)(2,1)S(1)}, bf16[32,3584]{1,0:T(8,128)(2,1)S(1)}, u32[]{:S(2)}, u32[]{:S(2)}) collective-permute-start(bf16[32,3584]{1,0:T(8,128)(2,1)S(1)} %shard_map.93), channel_id=1, source_target_pairs={{0,2},{1,3},{2,4},{3,5},{4,6},{5,7},{6,8},{7,9},{8,10},{9,11},{10,... | collective-permute-start | bytes 688136 | tf_op jit(solution)/shard_map/ppermute | solution.py:163
  326.3 11.9 %collective-permute-start.57 = (bf16[32,3584]{1,0:T(8,128)(2,1)S(1)}, bf16[32,3584]{1,0:T(8,128)(2,1)S(1)}, u32[]{:S(2)}, u32[]{:S(2)}) collective-permute-start(bf16[32,3584]{1,0:T(8,128)(2,1)S(1)} %shard_map.108), channel_id=1, source_target_pairs={{0,62},{1,63},{2,0},{3,1},{4,2},{5,3},{6,4},{7,5},{8,6},{9,7},{10,... | collective-permute-start | bytes 688136 | tf_op jit(solution)/shard_map/ppermute | solution.py:163
  331.0 10.6 %collective-permute-start.26 = (bf16[32,3584]{1,0:T(8,128)(2,1)S(1)}, bf16[32,3584]{1,0:T(8,128)(2,1)S(1)}, u32[]{:S(2)}, u32[]{:S(2)}) collective-permute-start(bf16[32,3584]{1,0:T(8,128)(2,1)S(1)} %shard_map.79), channel_id=1, source_target_pairs={{0,62},{1,63},{2,0},{3,1},{4,2},{5,3},{6,4},{7,5},{8,6},{9,7},{10,... | collective-permute-start | bytes 688136 | tf_op jit(solution)/shard_map/ppermute | solution.py:163
  334.3 10.6 %collective-permute-start.11 = (bf16[32,3584]{1,0:T(8,128)(2,1)S(1)}, bf16[32,3584]{1,0:T(8,128)(2,1)S(1)}, u32[]{:S(2)}, u32[]{:S(2)}) collective-permute-start(bf16[32,3584]{1,0:T(8,128)(2,1)S(1)} %shard_map.63), channel_id=1, source_target_pairs={{0,2},{1,3},{2,4},{3,5},{4,6},{5,7},{6,8},{7,9},{8,10},{9,11},{10,... | collective-permute-start | bytes 688136 | tf_op jit(solution)/shard_map/ppermute | solution.py:163
  338.0 9.0 %collective-permute-start.42 = (bf16[32,3584]{1,0:T(8,128)(2,1)S(1)}, bf16[32,3584]{1,0:T(8,128)(2,1)S(1)}, u32[]{:S(2)}, u32[]{:S(2)}) collective-permute-start(bf16[32,3584]{1,0:T(8,128)(2,1)S(1)} %shard_map.94), channel_id=1, source_target_pairs={{0,2},{1,3},{2,4},{3,5},{4,6},{5,7},{6,8},{7,9},{8,10},{9,11},{10,... | collective-permute-start | bytes 688136 | tf_op jit(solution)/shard_map/ppermute | solution.py:163
  347.4 15.6 %collective-permute-start.59 = (bf16[32,3584]{1,0:T(8,128)(2,1)S(1)}, bf16[32,3584]{1,0:T(8,128)(2,1)S(1)}, u32[]{:S(2)}, u32[]{:S(2)}) collective-permute-start(bf16[32,3584]{1,0:T(8,128)(2,1)S(1)} %shard_map.110), channel_id=1, source_target_pairs={{0,62},{1,63},{2,0},{3,1},{4,2},{5,3},{6,4},{7,5},{8,6},{9,7},{10,... | collective-permute-start | bytes 688136 | tf_op jit(solution)/shard_map/ppermute | solution.py:163
  350.7 15.8 %collective-permute-start.28 = (bf16[32,3584]{1,0:T(8,128)(2,1)S(1)}, bf16[32,3584]{1,0:T(8,128)(2,1)S(1)}, u32[]{:S(2)}, u32[]{:S(2)}) collective-permute-start(bf16[32,3584]{1,0:T(8,128)(2,1)S(1)} %shard_map.81), channel_id=1, source_target_pairs={{0,62},{1,63},{2,0},{3,1},{4,2},{5,3},{6,4},{7,5},{8,6},{9,7},{10,... | collective-permute-start | bytes 688136 | tf_op jit(solution)/shard_map/ppermute | solution.py:163
  352.8 13.9 %collective-permute-start.13 = (bf16[32,3584]{1,0:T(8,128)(2,1)S(1)}, bf16[32,3584]{1,0:T(8,128)(2,1)S(1)}, u32[]{:S(2)}, u32[]{:S(2)}) collective-permute-start(bf16[32,3584]{1,0:T(8,128)(2,1)S(1)} %shard_map.65), channel_id=1, source_target_pairs={{0,2},{1,3},{2,4},{3,5},{4,6},{5,7},{6,8},{7,9},{8,10},{9,11},{10,... | collective-permute-start | bytes 688136 | tf_op jit(solution)/shard_map/ppermute | solution.py:163
  355.3 13.6 %collective-permute-start.44 = (bf16[32,3584]{1,0:T(8,128)(2,1)S(1)}, bf16[32,3584]{1,0:T(8,128)(2,1)S(1)}, u32[]{:S(2)}, u32[]{:S(2)}) collective-permute-start(bf16[32,3584]{1,0:T(8,128)(2,1)S(1)} %shard_map.96), channel_id=1, source_target_pairs={{0,2},{1,3},{2,4},{3,5},{4,6},{5,7},{6,8},{7,9},{8,10},{9,11},{10,... | collective-permute-start | bytes 688136 | tf_op jit(solution)/shard_map/ppermute | solution.py:163
  363.0 9.2 %collective-permute-start.60 = (bf16[32,3584]{1,0:T(8,128)(2,1)S(1)}, bf16[32,3584]{1,0:T(8,128)(2,1)S(1)}, u32[]{:S(2)}, u32[]{:S(2)}) collective-permute-start(bf16[32,3584]{1,0:T(8,128)(2,1)S(1)} %shard_map.111), channel_id=1, source_target_pairs={{0,62},{1,63},{2,0},{3,1},{4,2},{5,3},{6,4},{7,5},{8,6},{9,7},{10,... | collective-permute-start | bytes 688136 | tf_op jit(solution)/shard_map/ppermute | solution.py:163
  366.6 10.6 %collective-permute-start.29 = (bf16[32,3584]{1,0:T(8,128)(2,1)S(1)}, bf16[32,3584]{1,0:T(8,128)(2,1)S(1)}, u32[]{:S(2)}, u32[]{:S(2)}) collective-permute-start(bf16[32,3584]{1,0:T(8,128)(2,1)S(1)} %shard_map.82), channel_id=1, source_target_pairs={{0,62},{1,63},{2,0},{3,1},{4,2},{5,3},{6,4},{7,5},{8,6},{9,7},{10,... | collective-permute-start | bytes 688136 | tf_op jit(solution)/shard_map/ppermute | solution.py:163
  366.8 14.2 %collective-permute-start.14 = (bf16[32,3584]{1,0:T(8,128)(2,1)S(1)}, bf16[32,3584]{1,0:T(8,128)(2,1)S(1)}, u32[]{:S(2)}, u32[]{:S(2)}) collective-permute-start(bf16[32,3584]{1,0:T(8,128)(2,1)S(1)} %shard_map.67), channel_id=1, source_target_pairs={{0,2},{1,3},{2,4},{3,5},{4,6},{5,7},{6,8},{7,9},{8,10},{9,11},{10,... | collective-permute-start | bytes 688136 | tf_op jit(solution)/shard_map/ppermute | solution.py:163
  369.0 12.5 %collective-permute-start.45 = (bf16[32,3584]{1,0:T(8,128)(2,1)S(1)}, bf16[32,3584]{1,0:T(8,128)(2,1)S(1)}, u32[]{:S(2)}, u32[]{:S(2)}) collective-permute-start(bf16[32,3584]{1,0:T(8,128)(2,1)S(1)} %shard_map.97), channel_id=1, source_target_pairs={{0,2},{1,3},{2,4},{3,5},{4,6},{5,7},{6,8},{7,9},{8,10},{9,11},{10,... | collective-permute-start | bytes 688136 | tf_op jit(solution)/shard_map/ppermute | solution.py:163
  372.3 9.4 %collective-permute-start.61 = (bf16[32,3584]{1,0:T(8,128)(2,1)S(1)}, bf16[32,3584]{1,0:T(8,128)(2,1)S(1)}, u32[]{:S(2)}, u32[]{:S(2)}) collective-permute-start(bf16[32,3584]{1,0:T(8,128)(2,1)S(1)} %shard_map.112), channel_id=1, source_target_pairs={{0,62},{1,63},{2,0},{3,1},{4,2},{5,3},{6,4},{7,5},{8,6},{9,7},{10,... | collective-permute-start | bytes 688136 | tf_op jit(solution)/shard_map/ppermute | solution.py:163
  377.2 9.8 %collective-permute-start.30 = (bf16[32,3584]{1,0:T(8,128)(2,1)S(1)}, bf16[32,3584]{1,0:T(8,128)(2,1)S(1)}, u32[]{:S(2)}, u32[]{:S(2)}) collective-permute-start(bf16[32,3584]{1,0:T(8,128)(2,1)S(1)} %shard_map.83), channel_id=1, source_target_pairs={{0,62},{1,63},{2,0},{3,1},{4,2},{5,3},{6,4},{7,5},{8,6},{9,7},{10,... | collective-permute-start | bytes 688136 | tf_op jit(solution)/shard_map/ppermute | solution.py:163
  381.1 9.8 %collective-permute-start.15 = (bf16[32,3584]{1,0:T(8,128)(2,1)S(1)}, bf16[32,3584]{1,0:T(8,128)(2,1)S(1)}, u32[]{:S(2)}, u32[]{:S(2)}) collective-permute-start(bf16[32,3584]{1,0:T(8,128)(2,1)S(1)} %shard_map.68), channel_id=1, source_target_pairs={{0,2},{1,3},{2,4},{3,5},{4,6},{5,7},{6,8},{7,9},{8,10},{9,11},{10,... | collective-permute-start | bytes 688136 | tf_op jit(solution)/shard_map/ppermute | solution.py:163
  381.6 13.8 %collective-permute-start.46 = (bf16[32,3584]{1,0:T(8,128)(2,1)S(1)}, bf16[32,3584]{1,0:T(8,128)(2,1)S(1)}, u32[]{:S(2)}, u32[]{:S(2)}) collective-permute-start(bf16[32,3584]{1,0:T(8,128)(2,1)S(1)} %shard_map.98), channel_id=1, source_target_pairs={{0,2},{1,3},{2,4},{3,5},{4,6},{5,7},{6,8},{7,9},{8,10},{9,11},{10,... | collective-permute-start | bytes 688136 | tf_op jit(solution)/shard_map/ppermute | solution.py:163
  381.8 13.7 %collective-permute-start.62 = (bf16[32,3584]{1,0:T(8,128)(2,1)S(1)}, bf16[32,3584]{1,0:T(8,128)(2,1)S(1)}, u32[]{:S(2)}, u32[]{:S(2)}) collective-permute-start(bf16[32,3584]{1,0:T(8,128)(2,1)S(1)} %shard_map.113), channel_id=1, source_target_pairs={{0,62},{1,63},{2,0},{3,1},{4,2},{5,3},{6,4},{7,5},{8,6},{9,7},{10,... | collective-permute-start | bytes 688136 | tf_op jit(solution)/shard_map/ppermute | solution.py:163
  387.1 11.9 %collective-permute-start.31 = (bf16[32,3584]{1,0:T(8,128)(2,1)S(1)}, bf16[32,3584]{1,0:T(8,128)(2,1)S(1)}, u32[]{:S(2)}, u32[]{:S(2)}) collective-permute-start(bf16[32,3584]{1,0:T(8,128)(2,1)S(1)} %shard_map.84), channel_id=1, source_target_pairs={{0,62},{1,63},{2,0},{3,1},{4,2},{5,3},{6,4},{7,5},{8,6},{9,7},{10,... | collective-permute-start | bytes 688136 | tf_op jit(solution)/shard_map/ppermute | solution.py:163
  395.4 9.8 %collective-permute-start.47 = (bf16[32,3584]{1,0:T(8,128)(2,1)S(1)}, bf16[32,3584]{1,0:T(8,128)(2,1)S(1)}, u32[]{:S(2)}, u32[]{:S(2)}) collective-permute-start(bf16[32,3584]{1,0:T(8,128)(2,1)S(1)} %shard_map.99), channel_id=1, source_target_pairs={{0,2},{1,3},{2,4},{3,5},{4,6},{5,7},{6,8},{7,9},{8,10},{9,11},{10,... | collective-permute-start | bytes 688136 | tf_op jit(solution)/shard_map/ppermute | solution.py:163
  395.6 17.5 %collective-permute-start.63 = (bf16[32,3584]{1,0:T(8,128)(2,1)S(1)}, bf16[32,3584]{1,0:T(8,128)(2,1)S(1)}, u32[]{:S(2)}, u32[]{:S(2)}) collective-permute-start(bf16[32,3584]{1,0:T(8,128)(2,1)S(1)} %shard_map.114), channel_id=1, source_target_pairs={{0,62},{1,63},{2,0},{3,1},{4,2},{5,3},{6,4},{7,5},{8,6},{9,7},{10,... | collective-permute-start | bytes 688136 | tf_op jit(solution)/shard_map/ppermute | solution.py:163
  399.0 17.5 %collective-permute-start.32 = (bf16[32,3584]{1,0:T(8,128)(2,1)S(1)}, bf16[32,3584]{1,0:T(8,128)(2,1)S(1)}, u32[]{:S(2)}, u32[]{:S(2)}) collective-permute-start(bf16[32,3584]{1,0:T(8,128)(2,1)S(1)} %shard_map.85), channel_id=1, source_target_pairs={{0,62},{1,63},{2,0},{3,1},{4,2},{5,3},{6,4},{7,5},{8,6},{9,7},{10,... | collective-permute-start | bytes 688136 | tf_op jit(solution)/shard_map/ppermute | solution.py:163
  399.2 17.5 %collective-permute-start.17 = (bf16[32,3584]{1,0:T(8,128)(2,1)S(1)}, bf16[32,3584]{1,0:T(8,128)(2,1)S(1)}, u32[]{:S(2)}, u32[]{:S(2)}) collective-permute-start(bf16[32,3584]{1,0:T(8,128)(2,1)S(1)} %shard_map.70), channel_id=1, source_target_pairs={{0,2},{1,3},{2,4},{3,5},{4,6},{5,7},{6,8},{7,9},{8,10},{9,11},{10,... | collective-permute-start | bytes 688136 | tf_op jit(solution)/shard_map/ppermute | solution.py:163
  405.3 13.7 %collective-permute-start.48 = (bf16[32,3584]{1,0:T(8,128)(2,1)S(1)}, bf16[32,3584]{1,0:T(8,128)(2,1)S(1)}, u32[]{:S(2)}, u32[]{:S(2)}) collective-permute-start(bf16[32,3584]{1,0:T(8,128)(2,1)S(1)} %shard_map.100), channel_id=1, source_target_pairs={{0,2},{1,3},{2,4},{3,5},{4,6},{5,7},{6,8},{7,9},{8,10},{9,11},{10,... | collective-permute-start | bytes 688136 | tf_op jit(solution)/shard_map/ppermute | solution.py:163
  416.8 12.4 %collective-permute-start.18 = (bf16[32,3584]{1,0:T(8,128)(2,1)S(1)}, bf16[32,3584]{1,0:T(8,128)(2,1)S(1)}, u32[]{:S(2)}, u32[]{:S(2)}) collective-permute-start(bf16[32,3584]{1,0:T(8,128)(2,1)S(1)} %shard_map.72), channel_id=1, source_target_pairs={{0,2},{1,3},{2,4},{3,5},{4,6},{5,7},{6,8},{7,9},{8,10},{9,11},{10,... | collective-permute-start | bytes 688136 | tf_op jit(solution)/shard_map/ppermute | solution.py:163
  419.0 12.2 %collective-permute-start.49 = (bf16[32,3584]{1,0:T(8,128)(2,1)S(1)}, bf16[32,3584]{1,0:T(8,128)(2,1)S(1)}, u32[]{:S(2)}, u32[]{:S(2)}) collective-permute-start(bf16[32,3584]{1,0:T(8,128)(2,1)S(1)} %shard_map.101), channel_id=1, source_target_pairs={{0,2},{1,3},{2,4},{3,5},{4,6},{5,7},{6,8},{7,9},{8,10},{9,11},{10,... | collective-permute-start | bytes 688136 | tf_op jit(solution)/shard_map/ppermute | solution.py:163
  420.5 10.9 %collective-permute-start.65 = (bf16[32,3584]{1,0:T(8,128)(2,1)S(1)}, bf16[32,3584]{1,0:T(8,128)(2,1)S(1)}, u32[]{:S(2)}, u32[]{:S(2)}) collective-permute-start(bf16[32,3584]{1,0:T(8,128)(2,1)S(1)} %shard_map.116), channel_id=1, source_target_pairs={{0,62},{1,63},{2,0},{3,1},{4,2},{5,3},{6,4},{7,5},{8,6},{9,7},{10,... | collective-permute-start | bytes 688136 | tf_op jit(solution)/shard_map/ppermute | solution.py:163
  425.4 9.4 %collective-permute-start.34 = (bf16[32,3584]{1,0:T(8,128)(2,1)S(1)}, bf16[32,3584]{1,0:T(8,128)(2,1)S(1)}, u32[]{:S(2)}, u32[]{:S(2)}) collective-permute-start(bf16[32,3584]{1,0:T(8,128)(2,1)S(1)} %shard_map.87), channel_id=1, source_target_pairs={{0,62},{1,63},{2,0},{3,1},{4,2},{5,3},{6,4},{7,5},{8,6},{9,7},{10,... | collective-permute-start | bytes 688136 | tf_op jit(solution)/shard_map/ppermute | solution.py:163
  (27 other events, 217.3 us)
